TPU v7x, 128 devices: a whole 4x4x4 slice. The times are simulated.
128 devices in a mesh: tm: 4 (over x), rows: 8 (over y, core), batch: 4 (over z).
Axes of the slice: x: 4, y: 4, z: 4, core: 2. Of those that a mesh axis runs over, the one named last changes fastest.
Arguments:
- inputs: bfloat16 [4, 8, 64, 128, 384], P('batch', 'tm', 'rows'), parts along dimension 0, may hold values from -16 to 16
- norm_gain: float32 [384], replicated, may hold values from 0.1 to 1.9
- norm_bias: float32 [384], replicated, may hold values from -3 to 3
- conv_weight: bfloat16 [3, 3, 3, 384, 384], replicated, may hold values from -0.0625 to 0.0625
- conv_bias: float32 [384], replicated, may hold values from -2 to 2
Outputs:
- decoded: bfloat16 [4, 8, 64, 128, 384], P('batch', 'tm', 'rows'), parts along dimension 0
There are 4 independent parts, one for each index of `batch`. A program takes and returns all parts, laid end to end along the dimension named above; an argument that names none is the same for every part. Nothing has to cross between parts.
All inputs are finite; a program needn't handle non-finite values.
Results may differ from a plain program's by a relative error of at most 0.0025.
Values may be sent and summed in bfloat16 or wider, within the bound.
A program may use at most 128 MiB of HBM per device.

v0:
```python
import jax
import jax.numpy as jnp
from jax import lax
from jax.sharding import PartitionSpec as P

GROUPS = 32


epsilon = 1e-06


def sent_to_all(x, axis):
    size = lax.axis_size(axis)
    return lax.all_to_all(jnp.broadcast_to(x[None], (size, *x.shape)), axis, 0, 0, tiled=True)


def over_copies(x, axis):
    return sent_to_all(x, axis).sum(axis=0)


def together(arrays, axis):
    line, at, gathered = (jnp.concatenate([a.reshape(-1) for a in arrays]), 0, [])
    subtotal = over_copies(line, axis)
    for a in arrays:
        gathered.append(subtotal[at : at + a.size].reshape(a.shape))
        at += a.size
    return tuple(gathered)


def with_halo(block, sides, width):
    for axis, dim in sides:
        count = lax.axis_size(axis)
        forward = [(i, i + 1) for i in range(count - 1)]
        backward = [(target, source) for source, target in forward]
        low = lax.ppermute(
            lax.slice_in_dim(block, block.shape[dim] - width, None, axis=dim), axis, forward
        )
        high = lax.ppermute(lax.slice_in_dim(block, 0, width, axis=dim), axis, backward)
        block = jnp.concatenate([low, block, high], axis=dim)
    return block


def from_behind(value, axis, steps):
    count = lax.axis_size(axis)
    initial, last = (max(0, -steps), min(count, count - steps))
    return lax.ppermute(value, axis, [(source, source + steps) for source in range(initial, last)])


def convolve(padded, conv_weight, frames, height, width_dev):
    channels = padded.shape[-1]
    summed = jnp.zeros(
        (padded.shape[0] * frames * height * width_dev, conv_weight.shape[-1]), jnp.float32
    )
    for tap_time in range(3):
        for tap_row in range(3):
            slab_rows = padded[:, tap_time : tap_time + frames, tap_row : tap_row + height]
            columns = jnp.concatenate(
                [
                    slab_rows[:, :, :, 0:width_dev],
                    slab_rows[:, :, :, 1 : width_dev + 1],
                    slab_rows[:, :, :, 2 : width_dev + 2],
                ],
                axis=-1,
            )
            kernel = conv_weight[tap_time, tap_row].reshape(3 * channels, -1)
            summed = summed + jnp.dot(
                columns.reshape(-1, 3 * channels), kernel, preferred_element_type=jnp.float32
            )
    return summed


def grouped(chan_values, per_group):
    return jnp.sum(chan_values.reshape(-1, per_group), axis=1)


def shards(inputs, norm_gain, norm_bias, conv_weight, conv_bias):
    values = inputs.astype(jnp.float32)
    clip_count, frames, height, width_dev, channels = inputs.shape
    per_group = channels // GROUPS
    cell_count = (
        1.0
        * clip_count
        * frames
        * height
        * width_dev
        * per_group
        * lax.axis_size("tm")
        * lax.axis_size("rows")
    )
    chan_sum = jnp.sum(values, axis=(0, 1, 2, 3))
    chan_raw = jnp.sum(values * values, axis=(0, 1, 2, 3))
    total_sum, total_square = together(
        (grouped(chan_sum, per_group), grouped(chan_raw, per_group)), ("tm", "rows")
    )
    group_mean = total_sum / cell_count
    group_var = total_square / cell_count - group_mean * group_mean
    centered = values - jnp.repeat(group_mean, per_group)
    inverse = jnp.repeat(lax.rsqrt(group_var + epsilon), per_group)
    normed = centered * inverse * norm_gain + norm_bias
    active = (normed * jax.nn.sigmoid(normed)).astype(jnp.bfloat16)
    rimmed = with_halo(active, (("rows", 2),), 1)
    earlier = from_behind(rimmed, "tm", 1)
    extended = jnp.concatenate([earlier, rimmed], axis=1)
    padded = jnp.pad(extended, ((0, 0), (0, 0), (0, 0), (1, 1), (0, 0)))
    summed = convolve(padded, conv_weight, frames, height, width_dev)
    result = values + summed.reshape(values.shape) + conv_bias
    return result.astype(jnp.bfloat16)


def solution(mesh):
    placed = (P("batch", "tm", "rows", None, None), P(), P(), P(), P())
    return jax.shard_map(
        shards,
        mesh=mesh,
        in_specs=placed,
        out_specs=P("batch", "tm", "rows", None, None),
        check_vma=False,
    )
```

profile of v0, /device:TPU:99, one launch (start us, length us, event | category | flops | bytes accessed | tf_op | source)
XLA Modules:
  0.0 142.7 jit_solution(12216313675691023717)
XLA Ops:
  0.0 1.9 %convert_reduce_fusion = (f32[384]{0:T(512)S(1)}, f32[384]{0:T(512)S(1)}) fusion(bf16[1,2,8,128,384]{4,3,2,1,0:T(8,128)(2,1)} %param.5), kind=kLoop, calls=%fused_computation.3 | loop fusion | flops 3144960 | bytes 1575936 | tf_op jit(solution)/shard_map/reduce_sum | solution.py:90
  1.9 0.1 reshape.57
  2.0 0.1 reshape.58
  2.1 0.1 reduce_sum.46
  2.2 0.1 reduce_sum.48
  2.3 0.1 pad_maximum_fusion.10
  2.4 13.7 %all_to_all.6 = f32[32,1,64]{2,1,0:T(1,128)S(1)} all-to-all(f32[32,1,64]{2,1,0:T(1,128)S(1)} %broadcast_in_dim.6), channel_id=1, replica_groups=mesh['tm'=4,'rows'=8,'batch'=4] {'tm','rows'}, dimensions={0} | all-to-all | bytes 16384 | tf_op jit(solution)/shard_map/all_to_all | solution.py:14
  16.1 0.1 slice_multiply_fusion
  16.2 0.1 broadcast_in_dim.8
  16.3 0.1 mul.29
  16.4 0.1 broadcast_in_dim.7
  16.4 0.1 sub.13
  16.6 2.5 %fusion.13 = bf16[1,2,8,128,384]{4,3,2,1,0:T(8,128)(2,1)S(1)} fusion(bf16[1,2,8,128,384]{4,3,2,1,0:T(8,128)(2,1)} %param.5, f32[384]{0:T(512)} %param.7, f32[384]{0:T(512)} %param.6, f32[384]{0:T(512)S(1)} %mul.29, f32[384]{0:T(512)S(1)} %sub.13), kind=kLoop, calls=%fused_computation.27 | loop fusion | flops 7864320 | bytes 3151872 | tf_op jit(solution)/shard_map/convert_element_type | solution.py:100
  19.1 2.7 %collective-permute-start = (bf16[1,2,1,128,384]{4,3,2,1,0:T(8,128)(2,1)S(1)}, bf16[1,2,1,128,384]{4,3,2,1,0:T(8,128)(2,1)S(1)}, u32[]{:S(2)}, u32[]{:S(2)}) collective-permute-start(bf16[1,2,1,128,384]{4,3,2,1,0:T(8,128)(2,1)S(1)} %get-tuple-element.42), channel_id=1, source_target_pairs={{0,4},{4,8},{8,12},{12,16},{16,20},{20,24},{24,28},{1,5},{5,9},{9,... | collective-permute-start | bytes 589832 | tf_op jit(solution)/shard_map/ppermute | solution.py:35
  21.9 1.9 %collective-permute-start.1 = (bf16[1,2,1,128,384]{4,3,2,1,0:T(8,128)(2,1)S(1)}, bf16[1,2,1,128,384]{4,3,2,1,0:T(8,128)(2,1)S(1)}, u32[]{:S(2)}, u32[]{:S(2)}) collective-permute-start(bf16[1,2,1,128,384]{4,3,2,1,0:T(8,128)(2,1)S(1)} %get-tuple-element.43), channel_id=1, source_target_pairs={{4,0},{8,4},{12,8},{16,12},{20,16},{24,20},{28,24},{5,1},{9,5},{13... | collective-permute-start | bytes 589832 | tf_op jit(solution)/shard_map/ppermute | solution.py:38
  23.8 0.7 collective-permute-done
  24.5 4.4 %collective-permute-done.1 = bf16[1,2,1,128,384]{4,3,2,1,0:T(8,128)(2,1)S(1)} collective-permute-done((bf16[1,2,1,128,384]{4,3,2,1,0:T(8,128)(2,1)S(1)}, bf16[1,2,1,128,384]{4,3,2,1,0:T(8,128)(2,1)S(1)}, u32[]{:S(2)}, u32[]{:S(2)}) %collective-permute-start.1) | collective-permute-done | bytes 196640 | tf_op jit(solution)/shard_map/ppermute | solution.py:38
  28.9 0.3 pad_maximum_fusion.9
  29.2 2.4 %collective-permute-start.2 = (bf16[1,2,10,128,384]{4,3,2,1,0:T(8,128)(2,1)S(1)}, bf16[1,2,10,128,384]{4,3,2,1,0:T(8,128)(2,1)S(1)}, u32[]{:S(2)}, u32[]{:S(2)}) collective-permute-start(bf16[1,2,10,128,384]{4,3,2,1,0:T(8,128)(2,1)S(1)} %pad_maximum_fusion.9), channel_id=1, source_target_pairs={{0,32},{32,64},{64,96},{1,33},{33,65},{65,97},{2,34},{34,66},{66,9... | collective-permute-start | bytes 5898248 | tf_op jit(solution)/shard_map/ppermute | solution.py:46
  31.6 5.7 %fusion.16 = (bf16[1,1,3,384,384]{4,3,2,1,0:T(8,128)(2,1)S(1)}, bf16[1,1,3,384,384]{4,3,2,1,0:T(8,128)(2,1)}, bf16[1,1,3,384,384]{4,3,2,1,0:T(8,128)(2,1)}, bf16...) fusion(bf16[3,3,3,384,384]{4,3,2,1,0:T(8,128)(2,1)} %param.8), kind=kLoop, calls=%fused_computation.53 | loop fusion | bytes 15925248 | tf_op jit(solution)/shard_map/slice | solution.py:65
  37.3 35.2 %collective-permute-done.2 = bf16[1,2,10,128,384]{4,3,2,1,0:T(8,128)(2,1)S(1)} collective-permute-done((bf16[1,2,10,128,384]{4,3,2,1,0:T(8,128)(2,1)S(1)}, bf16[1,2,10,128,384]{4,3,2,1,0:T(8,128)(2,1)S(1)}, u32[]{:S(2)}, u32[]{:S(2)}) %collective-permute-start.2) | collective-permute-done | bytes 1966112 | tf_op jit(solution)/shard_map/ppermute | solution.py:46
  72.4 0.0 copy-done.17
  72.5 0.6 maximum_maximum_fusion
  73.0 8.1 %pad_slice_fusion.1 = (bf16[1,2,8,128,384]{4,3,2,1,0:T(8,128)(2,1)}, bf16[1,2,8,128,384]{4,3,2,1,0:T(8,128)(2,1)}, bf16[1,2,8,128,384]{4,3,2,1,0:T(8,128)(2,1)},...) fusion(bf16[1,4,10,128,384]{4,3,2,1,0:T(8,128)(2,1)S(1)} %maxim, ...), kind=kLoop, calls=%fused_computation.36 | loop fusion | bytes 21233664 | tf_op jit(solution)/shard_map/slice | solution.py:59
  81.2 1.8 %pad_slice_fusion.17 = bf16[1,2,8,128,384]{4,3,2,1,0:T(8,128)(2,1)} fusion(bf16[1,4,10,128,384]{4,3,2,1,0:T(8,128)(2,1)S(1)} %maximum_maximum_fusion), kind=kLoop, calls=%fused_computation.52 | loop fusion | bytes 5505024 | tf_op jit(solution)/shard_map/slice | solution.py:59
  83.0 7.0 %pad_slice_fusion = (bf16[1,2,8,128,384]{4,3,2,1,0:T(8,128)(2,1)S(1)}, bf16[1,2,8,128,384]{4,3,2,1,0:T(8,128)(2,1)S(1)}, bf16[1,2,8,128,384]{4,3,2,1,0:T(8,128)(...) fusion(bf16[1,4,10,128,384]{4,3,2,1,0:T(8,128)(2,1)S(1)} %maxim, ...), kind=kLoop, calls=%fused_computation.35 | loop fusion | bytes 22806528 | tf_op jit(solution)/shard_map/slice | solution.py:61
  90.0 0.7 fusion.17
  90.8 0.6 copy-done.2
  91.4 0.5 copy-done.10
  91.9 0.5 copy-done.11
  92.4 0.5 copy-done.12
  92.9 1.1 pad_maximum_fusion.2
  94.0 0.1 copy-done.26
  94.0 4.5 %fusion.20 = f32[2048,384]{1,0:T(8,128)} fusion(bf16[2048,1152]{1,0:T(8,128)(2,1)S(1)} %bitcast.45, bf16[1152,384]{1,0:T(8,128)(2,1)S(1)} %bitcast.56), kind=kOutput, calls=%fused_computation.57 | convolution fusion | flops 1811939328 | bytes 8749056 | tf_op jit(solution)/shard_map/dot_general | solution.py:66
  98.5 0.0 copy-done.25
  98.6 4.4 %fusion.19 = f32[2048,384]{1,0:T(8,128)} fusion(bf16[2048,1152]{1,0:T(8,128)(2,1)S(1)} %bitcast.42, bf16[1152,384]{1,0:T(8,128)(2,1)S(1)} %bitcast.55), kind=kOutput, calls=%fused_computation.56 | convolution fusion | flops 1811939328 | bytes 8749056 | tf_op jit(solution)/shard_map/dot_general | solution.py:66
  103.0 1.3 pad_maximum_fusion.5
  104.3 2.8 %fusion.22 = f32[2048,384]{1,0:T(8,128)S(1)} fusion(bf16[2048,1152]{1,0:T(8,128)(2,1)S(1)} %bitcast.46, bf16[1152,384]{1,0:T(8,128)(2,1)S(1)} %bitcast.54), kind=kOutput, calls=%fused_computation.59 | convolution fusion | flops 1811939328 | bytes 8749056 | tf_op jit(solution)/shard_map/dot_general | solution.py:66
  107.2 4.5 %fusion.23 = f32[2048,384]{1,0:T(8,128)} fusion(bf16[2048,1152]{1,0:T(8,128)(2,1)S(1)} %bitcast.43, bf16[1152,384]{1,0:T(8,128)(2,1)S(1)} %bitcast.53), kind=kOutput, calls=%fused_computation.60 | convolution fusion | flops 1811939328 | bytes 8749056 | tf_op jit(solution)/shard_map/dot_general | solution.py:66
  111.7 1.1 pad_maximum_fusion.4
  112.8 0.1 copy-done.22
  112.9 4.5 %fusion.21 = f32[2048,384]{1,0:T(8,128)} fusion(bf16[2048,1152]{1,0:T(8,128)(2,1)S(1)} %bitcast.47, bf16[1152,384]{1,0:T(8,128)(2,1)S(1)} %bitcast.52), kind=kOutput, calls=%fused_computation.58 | convolution fusion | flops 1811939328 | bytes 8749056 | tf_op jit(solution)/shard_map/dot_general | solution.py:66
  117.4 4.4 %fusion.24 = f32[2048,384]{1,0:T(8,128)} fusion(bf16[2048,1152]{1,0:T(8,128)(2,1)S(1)} %bitcast.44, bf16[1152,384]{1,0:T(8,128)(2,1)S(1)} %bitcast.51), kind=kOutput, calls=%fused_computation.61 | convolution fusion | flops 1811939328 | bytes 8749056 | tf_op jit(solution)/shard_map/dot_general | solution.py:66
  121.8 2.5 %fusion.1 = (bf16[1,2,8,128,1152]{4,3,2,1,0:T(8,128)(2,1)S(1)}, bf16[1,2,8,128,1152]{4,3,2,1,0:T(8,128)(2,1)S(1)}, bf16[1,2,8,128,1152]{4,3,2,1,0:T(8,128)(2,1)S(1)}) fusion(bf16[1,2,1,128,384]{4,3,2,1,0:T(8,128)(2,1)S(1)} %copy-done.18, bf16[1,2,8,128,384]{4,3,2,1,0:T(8,128)(2,1)S(1)} %fusion.13, bf16[1,2,8,128,384]{4,3,2,1,0:T(8,128)(2,1)S(1)} %get-tuple-element.26, ...), kind=kLoop, calls=%fused_computation.6 | loop fusion | flops 51904512 | bytes 25559040 | tf_op jit(solution)/shard_map/concatenate | solution.py:57
  124.3 4.5 %fusion.25 = f32[2048,384]{1,0:T(8,128)} fusion(bf16[2048,1152]{1,0:T(8,128)(2,1)S(1)} %bitcast.41, bf16[1152,384]{1,0:T(8,128)(2,1)S(1)} %bitcast.50), kind=kOutput, calls=%fused_computation.62 | convolution fusion | flops 1811939328 | bytes 8749056 | tf_op jit(solution)/shard_map/dot_general | solution.py:66
  128.8 4.6 %fusion.26 = f32[2048,384]{1,0:T(8,128)} fusion(bf16[2048,1152]{1,0:T(8,128)(2,1)S(1)} %bitcast.40, bf16[1152,384]{1,0:T(8,128)(2,1)S(1)} %bitcast.49), kind=kOutput, calls=%fused_computation.63 | convolution fusion | flops 1811939328 | bytes 8749056 | tf_op jit(solution)/shard_map/dot_general | solution.py:66
  133.4 7.7 %add_add_fusion = f32[2048,384]{1,0:T(8,128)S(1)} fusion(f32[2048,384]{1,0:T(8,128)} %fusion.26, f32[2048,384]{1,0:T(8,128)} %fusion.25, f32[2048,384]{1,0:T(8,128)} %fusion.24, f32[2048,384]{1,0:T(8,128)} %fusion.23, f32[2048,384]{1,0:T(8,128)S(1)} %fusion.22, f32[2048,384]{1,0:T(8,128)} %fusion.21, f32[2048,384]{1,0:T(8,128)S(1)} %copy-done.14, ...), kind=kOutput, calls=%fused_computation.30 | convolution fusion | flops 1818230784 | bytes 33914880 | tf_op jit(solution)/shard_map/dot_general | solution.py:66
  141.1 1.6 %fusion.15 = bf16[1,2,8,128,384]{4,3,2,1,0:T(8,128)(2,1)} fusion(f32[1,2,8,128,384]{4,3,2,1,0:T(8,128)S(1)} %bitcast.39, bf16[1,2,8,128,384]{4,3,2,1,0:T(8,128)(2,1)S(1)} %copy-done, f32[384]{0:T(512)S(1)} %copy-done.27), kind=kLoop, calls=%fused_computation.29 | loop fusion | flops 3145728 | bytes 6292992 | tf_op jit(solution)/shard_map/convert_element_type | solution.py:107
  (51 shorter events, 0.2 us)
Async XLA Ops:
  19.1 5.3 %collective-permute-start = (bf16[1,2,1,128,384]{4,3,2,1,0:T(8,128)(2,1)S(1)}, bf16[1,2,1,128,384]{4,3,2,1,0:T(8,128)(2,1)S(1)}, u32[]{:S(2)}, u32[]{:S(2)}) collective-permute-start(bf16[1,2,1,128,384]{4,3,2,1,0:T(8,128)(2,1)S(1)} %get-tuple-element.42), channel_id=1, source_target_pairs={{0,4},{4,8},{8,12},{12,16},{16,20},{20,24},{24,28},{1,5},{5,9},{9,... | collective-permute-start | bytes 589832 | tf_op jit(solution)/shard_map/ppermute | solution.py:35
  21.9 7.0 %collective-permute-start.1 = (bf16[1,2,1,128,384]{4,3,2,1,0:T(8,128)(2,1)S(1)}, bf16[1,2,1,128,384]{4,3,2,1,0:T(8,128)(2,1)S(1)}, u32[]{:S(2)}, u32[]{:S(2)}) collective-permute-start(bf16[1,2,1,128,384]{4,3,2,1,0:T(8,128)(2,1)S(1)} %get-tuple-element.43), channel_id=1, source_target_pairs={{4,0},{8,4},{12,8},{16,12},{20,16},{24,20},{28,24},{5,1},{9,5},{13... | collective-permute-start | bytes 589832 | tf_op jit(solution)/shard_map/ppermute | solution.py:38
  24.5 48.0 %copy-start.15 = (bf16[1,2,1,128,384]{4,3,2,1,0:T(8,128)(2,1)}, bf16[1,2,1,128,384]{4,3,2,1,0:T(8,128)(2,1)S(1)}, u32[]{:S(2)}) copy-start(bf16[1,2,1,128,384]{4,3,2,1,0:T(8,128)(2,1)S(1)} %collective-permute-done) | copy-start | bytes 589828
  28.9 43.6 %copy-start.17 = (bf16[1,2,1,128,384]{4,3,2,1,0:T(8,128)(2,1)}, bf16[1,2,1,128,384]{4,3,2,1,0:T(8,128)(2,1)S(1)}, u32[]{:S(2)}) copy-start(bf16[1,2,1,128,384]{4,3,2,1,0:T(8,128)(2,1)S(1)} %collective-permute-done.1) | copy-start | bytes 589828
  29.2 43.3 %collective-permute-start.2 = (bf16[1,2,10,128,384]{4,3,2,1,0:T(8,128)(2,1)S(1)}, bf16[1,2,10,128,384]{4,3,2,1,0:T(8,128)(2,1)S(1)}, u32[]{:S(2)}, u32[]{:S(2)}) collective-permute-start(bf16[1,2,10,128,384]{4,3,2,1,0:T(8,128)(2,1)S(1)} %pad_maximum_fusion.9), channel_id=1, source_target_pairs={{0,32},{32,64},{64,96},{1,33},{33,65},{65,97},{2,34},{34,66},{66,9... | collective-permute-start | bytes 5898248 | tf_op jit(solution)/shard_map/ppermute | solution.py:46
  90.0 1.4 copy-start.2
  90.0 1.9 %copy-start.10 = (bf16[1,2,8,128,384]{4,3,2,1,0:T(8,128)(2,1)S(1)}, bf16[1,2,8,128,384]{4,3,2,1,0:T(8,128)(2,1)}, u32[]{:S(2)}) copy-start(bf16[1,2,8,128,384]{4,3,2,1,0:T(8,128)(2,1)} %get-tuple-element.17) | copy-start | bytes 4718596
  90.0 2.4 %copy-start.11 = (bf16[1,2,8,128,384]{4,3,2,1,0:T(8,128)(2,1)S(1)}, bf16[1,2,8,128,384]{4,3,2,1,0:T(8,128)(2,1)}, u32[]{:S(2)}) copy-start(bf16[1,2,8,128,384]{4,3,2,1,0:T(8,128)(2,1)} %get-tuple-element.18) | copy-start | bytes 4718596
  90.0 2.8 %copy-start.12 = (bf16[1,2,8,128,384]{4,3,2,1,0:T(8,128)(2,1)S(1)}, bf16[1,2,8,128,384]{4,3,2,1,0:T(8,128)(2,1)}, u32[]{:S(2)}) copy-start(bf16[1,2,8,128,384]{4,3,2,1,0:T(8,128)(2,1)} %get-tuple-element.19) | copy-start | bytes 4718596
  92.9 1.2 copy-start.26
  94.0 4.5 %copy-start.25 = (bf16[1,1,3,384,384]{4,3,2,1,0:T(8,128)(2,1)S(1)}, bf16[1,1,3,384,384]{4,3,2,1,0:T(8,128)(2,1)}, u32[]{:S(2)}) copy-start(bf16[1,1,3,384,384]{4,3,2,1,0:T(8,128)(2,1)} %get-tuple-element.14) | copy-start | bytes 2654212
  98.5 4.4 %copy-start.1 = (bf16[1,2,8,128,384]{4,3,2,1,0:T(8,128)(2,1)S(1)}, bf16[1,2,8,128,384]{4,3,2,1,0:T(8,128)(2,1)}, u32[]{:S(2)}) copy-start(bf16[1,2,8,128,384]{4,3,2,1,0:T(8,128)(2,1)} %get-tuple-element.35) | copy-start | bytes 4718596
  98.5 4.5 %copy-start.7 = (bf16[1,2,8,128,384]{4,3,2,1,0:T(8,128)(2,1)S(1)}, bf16[1,2,8,128,384]{4,3,2,1,0:T(8,128)(2,1)}, u32[]{:S(2)}) copy-start(bf16[1,2,8,128,384]{4,3,2,1,0:T(8,128)(2,1)} %get-tuple-element.22) | copy-start | bytes 4718596
  98.5 4.5 %copy-start.8 = (bf16[1,2,8,128,384]{4,3,2,1,0:T(8,128)(2,1)S(1)}, bf16[1,2,8,128,384]{4,3,2,1,0:T(8,128)(2,1)}, u32[]{:S(2)}) copy-start(bf16[1,2,8,128,384]{4,3,2,1,0:T(8,128)(2,1)} %get-tuple-element.23) | copy-start | bytes 4718596
  98.5 4.4 %copy-start.9 = (bf16[1,2,8,128,384]{4,3,2,1,0:T(8,128)(2,1)S(1)}, bf16[1,2,8,128,384]{4,3,2,1,0:T(8,128)(2,1)}, u32[]{:S(2)}) copy-start(bf16[1,2,8,128,384]{4,3,2,1,0:T(8,128)(2,1)} %get-tuple-element.24) | copy-start | bytes 4718596
  103.0 1.3 copy-start.24
  104.3 2.9 %copy-start.23 = (bf16[1,1,3,384,384]{4,3,2,1,0:T(8,128)(2,1)S(1)}, bf16[1,1,3,384,384]{4,3,2,1,0:T(8,128)(2,1)}, u32[]{:S(2)}) copy-start(bf16[1,1,3,384,384]{4,3,2,1,0:T(8,128)(2,1)} %get-tuple-element.10) | copy-start | bytes 2654212
  107.2 4.5 %copy-start.4 = (bf16[1,2,8,128,384]{4,3,2,1,0:T(8,128)(2,1)S(1)}, bf16[1,2,8,128,384]{4,3,2,1,0:T(8,128)(2,1)}, u32[]{:S(2)}) copy-start(bf16[1,2,8,128,384]{4,3,2,1,0:T(8,128)(2,1)} %get-tuple-element.20) | copy-start | bytes 4718596
  107.2 4.5 %copy-start.5 = (bf16[1,2,8,128,384]{4,3,2,1,0:T(8,128)(2,1)S(1)}, bf16[1,2,8,128,384]{4,3,2,1,0:T(8,128)(2,1)}, u32[]{:S(2)}) copy-start(bf16[1,2,8,128,384]{4,3,2,1,0:T(8,128)(2,1)} %get-tuple-element.21) | copy-start | bytes 4718596
  107.2 4.5 %copy-start.6 = (bf16[1,2,8,128,384]{4,3,2,1,0:T(8,128)(2,1)S(1)}, bf16[1,2,8,128,384]{4,3,2,1,0:T(8,128)(2,1)}, u32[]{:S(2)}) copy-start(bf16[1,2,8,128,384]{4,3,2,1,0:T(8,128)(2,1)} %get-tuple-element.25) | copy-start | bytes 4718596
  111.7 1.2 copy-start.22
  112.9 4.5 %copy-start.21 = (bf16[1,1,3,384,384]{4,3,2,1,0:T(8,128)(2,1)S(1)}, bf16[1,1,3,384,384]{4,3,2,1,0:T(8,128)(2,1)}, u32[]{:S(2)}) copy-start(bf16[1,1,3,384,384]{4,3,2,1,0:T(8,128)(2,1)} %get-tuple-element.9) | copy-start | bytes 2654212
  117.4 4.4 %copy-start.3 = (bf16[1,2,8,128,384]{4,3,2,1,0:T(8,128)(2,1)S(1)}, bf16[1,2,8,128,384]{4,3,2,1,0:T(8,128)(2,1)}, u32[]{:S(2)}) copy-start(bf16[1,2,8,128,384]{4,3,2,1,0:T(8,128)(2,1)} %get-tuple-element.16) | copy-start | bytes 4718596
  117.4 4.4 %copy-start.16 = (bf16[1,2,1,128,384]{4,3,2,1,0:T(8,128)(2,1)S(1)}, bf16[1,2,1,128,384]{4,3,2,1,0:T(8,128)(2,1)}, u32[]{:S(2)}) copy-start(bf16[1,2,1,128,384]{4,3,2,1,0:T(8,128)(2,1)} %copy-done.15) | copy-start | bytes 589828
  117.4 4.4 %copy-start.18 = (bf16[1,2,1,128,384]{4,3,2,1,0:T(8,128)(2,1)S(1)}, bf16[1,2,1,128,384]{4,3,2,1,0:T(8,128)(2,1)}, u32[]{:S(2)}) copy-start(bf16[1,2,1,128,384]{4,3,2,1,0:T(8,128)(2,1)} %copy-done.17) | copy-start | bytes 589828
  121.8 2.5 %copy-start.20 = (bf16[1,1,3,384,384]{4,3,2,1,0:T(8,128)(2,1)S(1)}, bf16[1,1,3,384,384]{4,3,2,1,0:T(8,128)(2,1)}, u32[]{:S(2)}) copy-start(bf16[1,1,3,384,384]{4,3,2,1,0:T(8,128)(2,1)} %get-tuple-element.8) | copy-start | bytes 2654212
  124.3 4.5 %copy-start.19 = (bf16[1,1,3,384,384]{4,3,2,1,0:T(8,128)(2,1)S(1)}, bf16[1,1,3,384,384]{4,3,2,1,0:T(8,128)(2,1)}, u32[]{:S(2)}) copy-start(bf16[1,1,3,384,384]{4,3,2,1,0:T(8,128)(2,1)} %get-tuple-element.15) | copy-start | bytes 2654212
  128.8 4.6 %copy-start.13 = (f32[2048,384]{1,0:T(8,128)S(1)}, f32[2048,384]{1,0:T(8,128)}, u32[]{:S(2)}) copy-start(f32[2048,384]{1,0:T(8,128)} %fusion.20) | copy-start | bytes 9437188
  128.8 4.6 %copy-start.14 = (f32[2048,384]{1,0:T(8,128)S(1)}, f32[2048,384]{1,0:T(8,128)}, u32[]{:S(2)}) copy-start(f32[2048,384]{1,0:T(8,128)} %fusion.19) | copy-start | bytes 9437188
  133.4 7.7 %copy-start = (bf16[1,2,8,128,384]{4,3,2,1,0:T(8,128)(2,1)S(1)}, bf16[1,2,8,128,384]{4,3,2,1,0:T(8,128)(2,1)}, u32[]{:S(2)}) copy-start(bf16[1,2,8,128,384]{4,3,2,1,0:T(8,128)(2,1)} %param.5) | copy-start | bytes 4718596
  133.4 7.7 %copy-start.27 = (f32[384]{0:T(512)S(1)}, f32[384]{0:T(512)}, u32[]{:S(2)}) copy-start(f32[384]{0:T(512)} %param.9) | copy-start | bytes 4612
where the time goes:
time: 145 us; the launch traced here: 143 us
  matrix products  41.9 us (29%)
  waiting for transfers between devices  40.2 us (28%)
  local copies, waits for them, and re-layouts  26.4 us (18%)
  blocking collectives  13.7 us (9%)
  other arithmetic  13.3 us (9%)
  starting transfers between devices  7.05 us (5%)
    dot_general x9, matrix products, convolve(): jnp.dot(columns.reshape(-1, 3 * channels), kernel, preferred_element_type...  41.9 us
    ppermute x1, waiting for transfers between devices, from_behind(): lax.ppermute(value, axis, [(source, source + steps) for source in range(i...  35.2 us
    all_to_all x1, blocking collectives, sent_to_all(): lax.all_to_all(jnp.broadcast_to(x[None], (size, *x.shape)), axis, 0, 0, t...  13.7 us
    slice x2, local copies, waits for them, and re-layouts, convolve(): slab_rows[:, :, :, 0:width_dev]  9.94 us
    slice x1, local copies, waits for them, and re-layouts, convolve(): slab_rows[:, :, :, 2:width_dev + 2]  7.05 us
    concatenate x4, other arithmetic, convolve(): jnp.concatenate([slab_rows[:, :, :, 0:width_dev], slab_rows[:, :, :, 1:wi...  5.97 us
    slice x1, local copies, waits for them, and re-layouts, convolve(): kernel = conv_weight[tap_time, tap_row].reshape(3 * channels, -1)  5.7 us
    ppermute x1, waiting for transfers between devices, with_halo(): lax.ppermute(lax.slice_in_dim(block, 0, width, axis=dim), axis, backward)  4.39 us
  transfers between devices with their start and end apart: 3, of which 3 were waited for; matrix products, arithmetic and copies ran while one was open for 4% of the time, Pallas kernels for 0%

commit v1 on v0

v1 whole, which is shorter than its diff:
```python
import functools

import jax
import jax.numpy as jnp
from jax import lax
from jax.experimental import pallas as pl
from jax.experimental.pallas import tpu as pltpu
from jax.sharding import PartitionSpec as P

MESH = pl.DeviceIdType.MESH
GROUPS = 32
EPS = 1e-06
F32 = jnp.float32
BF16 = jnp.bfloat16

PIECES = ((1, 0, 1), (1, 7, 1), (1, 1, 3), (1, 4, 3), (0, 0, 1), (0, 7, 1), (0, 1, 4), (0, 5, 2))


def kernel(
    cells, per_group,
    x, gain, bias, cbias, w, out,
    xo, xr, act, wv, z, ost, ind, tm_out, tm_in, row_out, row_in,
    load_sem, wsem, out_sem,
    bulk_send, bulk_recv, halo_send, halo_recv, fwd_send, fwd_recv,
    tm_send, tm_recv, row_send, row_recv,
):
    n_tm, n_rows = lax.axis_size("tm"), lax.axis_size("rows")
    j, r = lax.axis_index("tm"), lax.axis_index("rows")
    frames, height, width, ch = xo.shape[0], xo.shape[1] - 2, xo.shape[2], xo.shape[3]

    load = pltpu.make_async_copy(x.at[0], xo.at[:, 1 : height + 1], load_sem)
    load.start()
    wloads = [
        pltpu.make_async_copy(w.at[:, :, kw], wv.at[:, :, :, pl.ds(kw * ch, ch)], wsem.at[kw])
        for kw in range(3)
    ]
    for c in wloads:
        c.start()

    barrier = pltpu.get_barrier_semaphore()
    tm_peers = [{"tm": lax.rem(j + d, n_tm)} for d in range(1, n_tm)]
    row_peers = [{"rows": lax.rem(r + d, n_rows)} for d in range(1, n_rows)]
    for peer in tm_peers + row_peers:
        pl.semaphore_signal(barrier, inc=1, device_id=peer, device_id_type=MESH)
    pl.semaphore_wait(barrier, len(tm_peers) + len(row_peers))

    def bulk(i):
        f, first, rows = PIECES[i]
        return pltpu.make_async_remote_copy(
            src_ref=x.at[0, f, pl.ds(first, rows)],
            dst_ref=xr.at[f, pl.ds(1 + first, rows)],
            send_sem=bulk_send.at[i],
            recv_sem=bulk_recv.at[i],
            device_id={"tm": lax.rem(j + 1, n_tm)},
            device_id_type=MESH,
        )

    def edge(i, src, dst, ssem, rsem):
        return pltpu.make_async_remote_copy(
            src_ref=src, dst_ref=dst, send_sem=ssem, recv_sem=rsem,
            device_id={"rows": lax.rem(r + (n_rows - 1 if i == 0 else 1), n_rows)},
            device_id_type=MESH,
        )

    def own_edge(i):
        return edge(
            i, x.at[0, :, 0 if i == 0 else height - 1], xo.at[:, height + 1 if i == 0 else 0],
            halo_send.at[i], halo_recv.at[i],
        )

    def fwd_edge(f, i):
        return edge(
            i, xr.at[f, 1 if i == 0 else height], xr.at[f, height + 1 if i == 0 else 0],
            fwd_send.at[2 * f + i], fwd_recv.at[2 * f + i],
        )

    sends_on, recvs_on = j < n_tm - 1, j > 0
    up_on, down_on = r > 0, r < n_rows - 1

    @pl.when(sends_on)
    def _():
        bulk(0).start()
        bulk(1).start()

    @pl.when(up_on)
    def _():
        own_edge(0).start()

    @pl.when(down_on)
    def _():
        own_edge(1).start()

    a = lax.broadcasted_iota(jnp.int32, (ch, ch), 0)
    b = lax.broadcasted_iota(jnp.int32, (ch, ch), 1)
    group_of = lambda i: lax.shift_right_logical(i * 43691, 19)
    ind[...] = jnp.where(group_of(a) == group_of(b), 1.0, 0.0).astype(BF16)

    def over_group(v):
        hi = v.astype(BF16).astype(F32)
        mid = (v - hi).astype(BF16).astype(F32)
        lo = v - hi - mid
        parts = jnp.concatenate([hi, mid, lo, jnp.zeros_like(v)], axis=0).astype(BF16)
        got = jnp.dot(parts, ind[...], preferred_element_type=F32)
        return got[0:8] + (got[8:16] + got[16:24])

    load.wait()
    local = 1.0 * frames * height * width * per_group

    def fold(v):
        return jnp.sum(v.reshape(-1, 8, ch), axis=0)

    def all_rows(v):
        return jnp.broadcast_to(jnp.sum(v, axis=0, keepdims=True), (8, ch))

    def sum_body(i, acc):
        v = xo[lax.div(i, height), 1 + lax.rem(i, height)].astype(F32)
        return acc + fold(v)

    total = lax.fori_loop(0, frames * height, sum_body, jnp.zeros((8, ch), F32))
    mean = over_group(all_rows(total)) * (1.0 / local)

    def square_body(i, acc):
        v = xo[lax.div(i, height), 1 + lax.rem(i, height)].astype(F32)
        d = v - mean[0:1]
        return acc + fold(d * d)

    total = lax.fori_loop(0, frames * height, square_body, jnp.zeros((8, ch), F32))
    square = over_group(all_rows(total))

    top = lax.broadcasted_iota(jnp.int32, (8, ch), 0) == 0

    def exchange(mean, square, count, axis, peers, index, outbox, inbox, ssem, rsem):
        size = len(peers) + 1
        outbox[...] = jnp.where(top, mean, square)
        copies = [
            pltpu.make_async_remote_copy(
                src_ref=outbox, dst_ref=inbox.at[d], send_sem=ssem.at[d], recv_sem=rsem.at[d],
                device_id=peers[d], device_id_type=MESH,
            )
            for d in range(size - 1)
        ]
        for c in copies:
            c.start()
        for c in copies:
            c.wait()
        got = [inbox[d] for d in range(size - 1)]
        means = [mean[0:1]] + [g[0:1] for g in got]
        whole = sum(means) * (1.0 / size)
        squares = square[0:1] + sum(g[1:2] for g in got)
        for m in means:
            squares = squares + count * ((m - whole) * (m - whole))
        return jnp.broadcast_to(whole, (8, ch)), jnp.broadcast_to(squares, (8, ch))

    mean, square = exchange(mean, square, local, "tm", tm_peers, j, tm_out, tm_in, tm_send, tm_recv)

    @pl.when(sends_on)
    def _():
        for i in range(2, len(PIECES)):
            bulk(i).start()

    mean, square = exchange(
        mean, square, local * n_tm, "rows", row_peers, r, row_out, row_in, row_send, row_recv
    )
    inverse = lax.rsqrt(square[0:1] * (1.0 / cells) + EPS)
    mean = mean[0:1]
    scale = 0.5 * (inverse * gain[...])
    shift = 0.5 * bias[...]

    def activate(v):
        h = (v.astype(F32) - mean) * scale + shift
        return (h + h * jnp.tanh(h)).astype(BF16)

    def normalize(src, f, dst, first, count):
        def body(i, _):
            act[dst, first + i] = activate(src[f, first + i])
            return 0

        lax.fori_loop(0, count, body, 0)

    def normalize_edges(src, f, dst):
        for on, row in ((up_on, 0), (down_on, height + 1)):

            @pl.when(on)
            def _():
                act[dst, row] = activate(src[f, row])

            @pl.when(jnp.logical_not(on))
            def _():
                act[dst, row] = jnp.zeros((width, ch), BF16)

    def product(t, used, kt, first, rows, add):
        m, k = rows * width, 3 * ch
        lhs = jnp.concatenate(
            [act[f, pl.ds(first + kh, rows)].reshape(m, ch) for f in used for kh in range(3)], axis=1
        )
        for lo in range(0, 3 * ch, 256):
            n = min(256, 3 * ch - lo)
            rhs = wv[pl.ds(kt, len(used)), :, :, pl.ds(lo, n)].reshape(len(used) * k, n)
            got = jnp.dot(lhs, rhs, preferred_element_type=F32).reshape(rows, width, n)
            at = (t, pl.ds(first, rows), slice(None), pl.ds(lo, n))
            z[at] = z[at] + got if add else got

    wi = lax.broadcasted_iota(jnp.int32, (width, ch), 0)

    def finish(t, first, rows):
        def body(i, _):
            h = first + i
            left = pltpu.roll(z[t, h, :, 0:ch], 1, 0)
            right = pltpu.roll(z[t, h, :, 2 * ch : 3 * ch], width - 1, 0)
            conv = z[t, h, :, ch : 2 * ch]
            conv = conv + jnp.where(wi == 0, 0.0, left) + jnp.where(wi == width - 1, 0.0, right)
            ost[t, h] = (xo[t, h + 1].astype(F32) + conv + cbias[...]).astype(BF16)
            return 0

        lax.fori_loop(0, rows, body, 0)

    def output(t, first, rows, i):
        return pltpu.make_async_copy(
            ost.at[t, pl.ds(first, rows)], out.at[0, t, pl.ds(first, rows)], out_sem.at[i]
        )

    for f in range(frames):
        normalize(xo, f, 2 + f, 1, height)

    @pl.when(down_on)
    def _():
        own_edge(0).wait_recv()

    @pl.when(up_on)
    def _():
        own_edge(1).wait_recv()

    for f in range(frames):
        normalize_edges(xo, f, 2 + f)

    def forward(f):
        @pl.when(recvs_on)
        def _():
            a, b = [i for i, p in enumerate(PIECES) if p[0] == f][:2]
            bulk(a).wait_recv()
            bulk(b).wait_recv()

            @pl.when(up_on)
            def _():
                fwd_edge(f, 0).start()

            @pl.when(down_on)
            def _():
                fwd_edge(f, 1).start()

    forward(1)
    for c in wloads:
        c.wait()

    half = height // 2

    @pl.loop(0, 2)
    def _(i):
        product(0, (2,), 2, i * half, half, False)
        product(1, (2, 3), 1, i * half, half, False)

    def edges_in(f):
        @pl.when(down_on)
        def _():
            fwd_edge(f, 0).wait_recv()

        @pl.when(up_on)
        def _():
            fwd_edge(f, 1).wait_recv()

    forward(0)

    @pl.when(recvs_on)
    def _():
        edges_in(1)
        for i in (2, 3):
            bulk(i).wait_recv()
        normalize(xr, 1, 1, 1, height)
        normalize_edges(xr, 1, 1)

        @pl.loop(0, 2)
        def _(i):
            product(0, (1,), 1, i * half, half, True)
            product(1, (1,), 0, i * half, half, True)

    finish(1, 0, height)
    output(1, 0, height, 0).start()

    @pl.when(recvs_on)
    def _():
        edges_in(0)
        normalize_edges(xr, 0, 0)
        bulk(6).wait_recv()
        normalize(xr, 0, 0, 1, 5)
        normalize(xr, 0, 0, 8, 1)
        product(0, (0,), 0, 0, half, True)

    finish(0, 0, half)
    output(0, 0, half, 1).start()

    @pl.when(recvs_on)
    def _():
        bulk(7).wait_recv()
        normalize(xr, 0, 0, 6, 2)
        product(0, (0,), 0, half, half, True)

    finish(0, half, half)
    output(0, half, half, 2).start()

    @pl.when(sends_on)
    def _():
        for i in range(len(PIECES)):
            bulk(i).wait_send()

    for i, on in ((0, up_on), (1, down_on)):

        @pl.when(on)
        def _():
            own_edge(i).wait_send()

            @pl.when(recvs_on)
            def _():
                for f in range(2):
                    fwd_edge(f, i).wait_send()

    output(1, 0, height, 0).wait()
    output(0, 0, half, 1).wait()
    output(0, half, half, 2).wait()


def shards(inputs, norm_gain, norm_bias, conv_weight, conv_bias):
    clips, frames, height, width, ch = inputs.shape
    n_tm, n_rows = lax.axis_size("tm"), lax.axis_size("rows")
    per_group = ch // GROUPS
    cells = 1.0 * clips * frames * height * width * per_group * n_tm * n_rows
    any_space = pl.BlockSpec(memory_space=pl.ANY)
    vmem = pl.BlockSpec(memory_space=pltpu.VMEM)
    dma = lambda n: pltpu.SemaphoreType.DMA((n,))
    return pl.pallas_call(
        functools.partial(kernel, cells, per_group),
        out_shape=jax.ShapeDtypeStruct(inputs.shape, BF16),
        in_specs=[any_space, vmem, vmem, vmem, any_space],
        out_specs=any_space,
        scratch_shapes=[
            pltpu.VMEM((frames, height + 2, width, ch), BF16),
            pltpu.VMEM((2, height + 2, width, ch), BF16),
            pltpu.VMEM((frames + 2, height + 2, width, ch), BF16),
            pltpu.VMEM((3, 3, ch, 3 * ch), BF16),
            pltpu.VMEM((frames, height, width, 3 * ch), F32),
            pltpu.VMEM((frames, height, width, ch), BF16),
            pltpu.VMEM((ch, ch), BF16),
            pltpu.VMEM((8, ch), F32),
            pltpu.VMEM((n_tm - 1, 8, ch), F32),
            pltpu.VMEM((8, ch), F32),
            pltpu.VMEM((n_rows - 1, 8, ch), F32),
            pltpu.SemaphoreType.DMA,
            dma(3),
            dma(3),
            dma(len(PIECES)),
            dma(len(PIECES)),
            dma(2),
            dma(2),
            dma(4),
            dma(4),
            dma(n_tm - 1),
            dma(n_tm - 1),
            dma(n_rows - 1),
            dma(n_rows - 1),
        ],
        compiler_params=pltpu.CompilerParams(
            collective_id=0, has_side_effects=True, vmem_limit_bytes=60 * 1024 * 1024
        ),
    )(
        inputs,
        norm_gain.reshape(1, ch),
        norm_bias.reshape(1, ch),
        conv_bias.reshape(1, ch),
        conv_weight,
    )


def solution(mesh):
    placed = (P("batch", "tm", "rows", None, None), P(), P(), P(), P())
    return jax.shard_map(
        shards,
        mesh=mesh,
        in_specs=placed,
        out_specs=P("batch", "tm", "rows", None, None),
        check_vma=False,
    )
```

time: 145 us -> 53.4 us (0.37)
  the two profiles are of different devices: /device:TPU:99 before, /device:TPU:66 now
where the time goes in v1:
time: 53.4 us; the launch traced here: 53.2 us
  Pallas kernels  46.6 us (87%)
  local copies, waits for them, and re-layouts  6.52 us (12%)
    pallas_call x1, Pallas kernels, shards(): pl.pallas_call(functools.partial(kernel, cells, per_group), out_shape=jax...  46.6 us
    unnamed x1, local copies, waits for them, and re-layouts  2.76 us
    reshape x1, local copies, waits for them, and re-layouts, shards(): conv_bias.reshape(1, ch)  1.26 us
    reshape x1, local copies, waits for them, and re-layouts, shards(): norm_bias.reshape(1, ch)  1.25 us
    reshape x1, local copies, waits for them, and re-layouts, shards(): norm_gain.reshape(1, ch)  1.24 us

profile of v1, /device:TPU:66, one launch (start us, length us, event | category | flops | bytes accessed | tf_op | source)
XLA Modules:
  0.0 53.2 jit_solution(7883759146335771155)
XLA Ops:
  0.0 1.2 %reshape.9.gain = f32[1,384]{1,0:T(1,128)} reshape(f32[384]{0:T(512)} %param.6) | data formatting | bytes 3072 | tf_op jit(solution)/shard_map/reshape | solution.py:375
  1.2 1.3 %reshape.10.bias = f32[1,384]{1,0:T(1,128)} reshape(f32[384]{0:T(512)} %param.7) | data formatting | bytes 3072 | tf_op jit(solution)/shard_map/reshape | solution.py:376
  2.5 1.3 %reshape.11.cbias = f32[1,384]{1,0:T(1,128)} reshape(f32[384]{0:T(512)} %param.9) | data formatting | bytes 3072 | tf_op jit(solution)/shard_map/reshape | solution.py:377
  3.8 46.6 %shard_map.55 = bf16[1,2,8,128,384]{4,3,2,1,0:T(8,128)(2,1)} custom-call(bf16[1,2,8,128,384]{4,3,2,1,0:T(8,128)(2,1)} %x.1, f32[1,384]{1,0:T(1,128)} %reshape.9.gain, f32[1,384]{1,0:T(1,128)} %reshape.10.bias, f32[1,384]{1,0:T(1,128)} %reshape.11.cbias, bf16[3,3,3,384,384]{4,3,2,1,0:T(8,128)(2,1)} %w.1), custom_call_target="tpu_custom_call" | custom-call | tf_op jit(solution)/shard_map/pallas_call | solution.py:339
  50.4 2.8 %copy.7 = bf16[1,2,8,128,384]{4,3,2,1,0:T(8,128)(2,1)} copy(bf16[1,2,8,128,384]{4,3,2,1,0:T(8,128)(2,1)} %shard_map.55) | data formatting | bytes 3145728

commit v2 on v1

--- a/solution.py
+++ b/solution.py
@@ -18,9 +18,9 @@
 
 def kernel(
     cells, per_group,
-    x, gain, bias, cbias, w, out,
+    x, vec, w, out,
     xo, xr, act, wv, z, ost, ind, tm_out, tm_in, row_out, row_in,
-    load_sem, wsem, out_sem,
+    gv, load_sem, wsem, out_sem, vec_sem,
     bulk_send, bulk_recv, halo_send, halo_recv, fwd_send, fwd_recv,
     tm_send, tm_recv, row_send, row_recv,
 ):
@@ -35,6 +35,9 @@
         for kw in range(3)
     ]
     for c in wloads:
+        c.start()
+    vectors = [pltpu.make_async_copy(vec, gv, vec_sem)]
+    for c in vectors:
         c.start()
 
     barrier = pltpu.get_barrier_semaphore()
@@ -104,6 +107,8 @@
         return got[0:8] + (got[8:16] + got[16:24])
 
     load.wait()
+    for c in vectors:
+        c.wait()
     local = 1.0 * frames * height * width * per_group
 
     def fold(v):
@@ -129,7 +134,7 @@
 
     top = lax.broadcasted_iota(jnp.int32, (8, ch), 0) == 0
 
-    def exchange(mean, square, count, axis, peers, index, outbox, inbox, ssem, rsem):
+    def exchange(mean, square, count, peers, outbox, inbox, ssem, rsem, between):
         size = len(peers) + 1
         outbox[...] = jnp.where(top, mean, square)
         copies = [
@@ -141,6 +146,7 @@
         ]
         for c in copies:
             c.start()
+        between()
         for c in copies:
             c.wait()
         got = [inbox[d] for d in range(size - 1)]
@@ -151,20 +157,22 @@
             squares = squares + count * ((m - whole) * (m - whole))
         return jnp.broadcast_to(whole, (8, ch)), jnp.broadcast_to(squares, (8, ch))
 
-    mean, square = exchange(mean, square, local, "tm", tm_peers, j, tm_out, tm_in, tm_send, tm_recv)
-
-    @pl.when(sends_on)
-    def _():
-        for i in range(2, len(PIECES)):
-            bulk(i).start()
+    def rest_of_bulk():
+        @pl.when(sends_on)
+        def _():
+            for i in range(2, len(PIECES)):
+                bulk(i).start()
 
     mean, square = exchange(
-        mean, square, local * n_tm, "rows", row_peers, r, row_out, row_in, row_send, row_recv
+        mean, square, local, tm_peers, tm_out, tm_in, tm_send, tm_recv, rest_of_bulk
+    )
+    mean, square = exchange(
+        mean, square, local * n_tm, row_peers, row_out, row_in, row_send, row_recv, lambda: None
     )
     inverse = lax.rsqrt(square[0:1] * (1.0 / cells) + EPS)
     mean = mean[0:1]
-    scale = 0.5 * (inverse * gain[...])
-    shift = 0.5 * bias[...]
+    scale = 0.5 * (inverse * gv[pl.ds(0 * ch, ch)].reshape(1, ch))
+    shift = 0.5 * gv[pl.ds(1 * ch, ch)].reshape(1, ch)
 
     def activate(v):
         h = (v.astype(F32) - mean) * scale + shift
@@ -209,7 +217,7 @@
             right = pltpu.roll(z[t, h, :, 2 * ch : 3 * ch], width - 1, 0)
             conv = z[t, h, :, ch : 2 * ch]
             conv = conv + jnp.where(wi == 0, 0.0, left) + jnp.where(wi == width - 1, 0.0, right)
-            ost[t, h] = (xo[t, h + 1].astype(F32) + conv + cbias[...]).astype(BF16)
+            out[0, t, h] = (xo[t, h + 1].astype(F32) + conv + gv[pl.ds(2 * ch, ch)].reshape(1, ch)).astype(BF16)
             return 0
 
         lax.fori_loop(0, rows, body, 0)
@@ -284,7 +292,6 @@
             product(1, (1,), 0, i * half, half, True)
 
     finish(1, 0, height)
-    output(1, 0, height, 0).start()
 
     @pl.when(recvs_on)
     def _():
@@ -296,7 +303,6 @@
         product(0, (0,), 0, 0, half, True)
 
     finish(0, 0, half)
-    output(0, 0, half, 1).start()
 
     @pl.when(recvs_on)
     def _():
@@ -305,7 +311,6 @@
         product(0, (0,), 0, half, half, True)
 
     finish(0, half, half)
-    output(0, half, half, 2).start()
 
     @pl.when(sends_on)
     def _():
@@ -322,10 +327,6 @@
             def _():
                 for f in range(2):
                     fwd_edge(f, i).wait_send()
-
-    output(1, 0, height, 0).wait()
-    output(0, 0, half, 1).wait()
-    output(0, half, half, 2).wait()
 
 
 def shards(inputs, norm_gain, norm_bias, conv_weight, conv_bias):
@@ -333,14 +334,13 @@
     n_tm, n_rows = lax.axis_size("tm"), lax.axis_size("rows")
     per_group = ch // GROUPS
     cells = 1.0 * clips * frames * height * width * per_group * n_tm * n_rows
-    any_space = pl.BlockSpec(memory_space=pl.ANY)
-    vmem = pl.BlockSpec(memory_space=pltpu.VMEM)
+    any_space = pl.BlockSpec(memory_space=pltpu.HBM)
     dma = lambda n: pltpu.SemaphoreType.DMA((n,))
     return pl.pallas_call(
         functools.partial(kernel, cells, per_group),
         out_shape=jax.ShapeDtypeStruct(inputs.shape, BF16),
-        in_specs=[any_space, vmem, vmem, vmem, any_space],
-        out_specs=any_space,
+        in_specs=[any_space] * 3,
+        out_specs=pl.BlockSpec(memory_space=pltpu.VMEM),
         scratch_shapes=[
             pltpu.VMEM((frames, height + 2, width, ch), BF16),
             pltpu.VMEM((2, height + 2, width, ch), BF16),
@@ -353,9 +353,11 @@
             pltpu.VMEM((n_tm - 1, 8, ch), F32),
             pltpu.VMEM((8, ch), F32),
             pltpu.VMEM((n_rows - 1, 8, ch), F32),
+            pltpu.VMEM((3 * ch,), F32),
             pltpu.SemaphoreType.DMA,
             dma(3),
             dma(3),
+            pltpu.SemaphoreType.DMA,
             dma(len(PIECES)),
             dma(len(PIECES)),
             dma(2),
@@ -368,13 +370,11 @@
             dma(n_rows - 1),
         ],
         compiler_params=pltpu.CompilerParams(
-            collective_id=0, has_side_effects=True, vmem_limit_bytes=60 * 1024 * 1024
+            collective_id=0, has_side_effects=True, vmem_limit_bytes=51 * 1024 * 1024
         ),
     )(
         inputs,
-        norm_gain.reshape(1, ch),
-        norm_bias.reshape(1, ch),
-        conv_bias.reshape(1, ch),
+        jnp.concatenate([norm_gain, norm_bias, conv_bias]),
         conv_weight,
     )
 

time: 53.4 us -> 44.2 us (0.83)
  the two profiles are of different devices: /device:TPU:66 before, /device:TPU:99 now
where the time goes in v2:
time: 44.2 us; the launch traced here: 43.5 us
  Pallas kernels  41.7 us (94%)
  local copies, waits for them, and re-layouts  1.15 us (3%)
  other arithmetic  0.72 us (2%)
    pallas_call x1, Pallas kernels, shards(): pl.pallas_call(functools.partial(kernel, cells, per_group), out_shape=jax...  41.7 us
    unnamed x1, local copies, waits for them, and re-layouts  1.15 us

profile of v2, /device:TPU:99, one launch (start us, length us, event | category | flops | bytes accessed | tf_op | source)
XLA Modules:
  0.0 43.5 jit_solution(9280056743999973545)
XLA Ops:
  0.0 0.7 %pad_maximum_fusion.vec = f32[1152]{0:T(1024)S(1)} fusion(f32[384]{0:T(512)} %param.9, f32[384]{0:T(512)} %param.7, f32[384]{0:T(512)} %param.6), kind=kLoop, calls=%fused_computation | loop fusion | flops 2304 | bytes 9216 | tf_op jit(solution)/shard_map/concatenate | solution.py:377
  0.7 41.7 %shard_map.55 = bf16[1,2,8,128,384]{4,3,2,1,0:T(8,128)(2,1)S(1)} custom-call(bf16[1,2,8,128,384]{4,3,2,1,0:T(8,128)(2,1)} %x.1, f32[1152]{0:T(1024)S(1)} %pad_maximum_fusion.vec, bf16[3,3,3,384,384]{4,3,2,1,0:T(8,128)(2,1)} %w.1), custom_call_target="tpu_custom_call" | custom-call | tf_op jit(solution)/shard_map/pallas_call | solution.py:339
  42.4 1.1 %copy.7 = bf16[1,2,8,128,384]{4,3,2,1,0:T(8,128)(2,1)} copy(bf16[1,2,8,128,384]{4,3,2,1,0:T(8,128)(2,1)S(1)} %shard_map.55) | data formatting | bytes 3145728

commit v3 on v2

v3 whole, which is shorter than its diff:
```python
import functools

import jax
import jax.numpy as jnp
from jax import lax
from jax.experimental import pallas as pl
from jax.experimental.pallas import tpu as pltpu
from jax.sharding import PartitionSpec as P

MESH = pl.DeviceIdType.MESH
GROUPS = 32
EPS = 1e-06
F32 = jnp.float32
BF16 = jnp.bfloat16

PIECES = ((1, 0, 1), (1, 7, 1), (1, 1, 4), (1, 5, 2), (0, 0, 1), (0, 7, 1), (0, 1, 2), (0, 6, 1))
BACK = (3, 3)


def kernel(
    cells, per_group,
    x, vec, w, out,
    xo, xr, act_a, act_b, act_c, act_d, wv, z, ind, tm_out, tm_in, row_out, row_in, hop1, hop2, gv,
    load_sem, wsem, vec_sem,
    bulk_send, bulk_recv, back_send, back_recv, halo_send, halo_recv, fwd_send, fwd_recv,
    tm_send, tm_recv, row_send, row_recv,
):
    n_tm, n_rows = lax.axis_size("tm"), lax.axis_size("rows")
    j, r = lax.axis_index("tm"), lax.axis_index("rows")
    frames, height, width, ch = xo.shape[0], xo.shape[1] - 2, xo.shape[2], xo.shape[3]
    half = height // 2

    load = pltpu.make_async_copy(x.at[0], xo.at[:, 1 : height + 1], load_sem)
    load.start()
    vector = pltpu.make_async_copy(vec, gv, vec_sem)
    vector.start()
    wloads = [
        pltpu.make_async_copy(w.at[:, :, kw], wv.at[:, :, :, pl.ds(kw * ch, ch)], wsem.at[kw])
        for kw in range(3)
    ]
    for c in wloads:
        c.start()

    barrier = pltpu.get_barrier_semaphore()
    tm_peers = [{"tm": lax.rem(j + d, n_tm)} for d in range(1, n_tm)]
    row_peers = [{"rows": lax.rem(r + d, n_rows)} for d in range(1, n_rows)]
    for peer in tm_peers + row_peers:
        pl.semaphore_signal(barrier, inc=1, device_id=peer, device_id_type=MESH)

    def bulk(i):
        f, first, rows = PIECES[i]
        return pltpu.make_async_remote_copy(
            src_ref=x.at[0, f, pl.ds(first, rows)],
            dst_ref=xr.at[f, pl.ds(1 + first, rows)],
            send_sem=bulk_send.at[i],
            recv_sem=bulk_recv.at[i],
            device_id={"tm": lax.rem(j + 1, n_tm)},
            device_id_type=MESH,
        )

    def back(i):
        first, rows = BACK
        src, dst = (
            (x.at[0, 0, pl.ds(first, rows)], hop1),
            (hop1, hop2),
            (hop2, xr.at[0, pl.ds(1 + first, rows)]),
        )[i]
        return pltpu.make_async_remote_copy(
            src_ref=src, dst_ref=dst, send_sem=back_send.at[i], recv_sem=back_recv.at[i],
            device_id={"tm": lax.rem(j + n_tm - 1, n_tm)}, device_id_type=MESH,
        )

    def edge(i, src, dst, ssem, rsem):
        return pltpu.make_async_remote_copy(
            src_ref=src, dst_ref=dst, send_sem=ssem, recv_sem=rsem,
            device_id={"rows": lax.rem(r + (n_rows - 1 if i == 0 else 1), n_rows)},
            device_id_type=MESH,
        )

    def own_edge(i):
        return edge(
            i, x.at[0, :, 0 if i == 0 else height - 1], xo.at[:, height + 1 if i == 0 else 0],
            halo_send.at[i], halo_recv.at[i],
        )

    def fwd_edge(f, i):
        return edge(
            i, xr.at[f, 1 if i == 0 else height], xr.at[f, height + 1 if i == 0 else 0],
            fwd_send.at[2 * f + i], fwd_recv.at[2 * f + i],
        )

    sends_on, recvs_on = j < n_tm - 1, j > 0
    second_on, third_on = j != n_tm - 2, j != n_tm - 3
    up_on, down_on = r > 0, r < n_rows - 1

    @pl.when(jnp.logical_not(recvs_on))
    def _():
        xr[...] = jnp.zeros_like(xr)

    for on, row in ((up_on, 0), (down_on, height + 1)):

        @pl.when(jnp.logical_not(on))
        def _():
            xo[:, row] = jnp.zeros((frames, width, ch), BF16)
            xr[:, row] = jnp.zeros((2, width, ch), BF16)

    a = lax.broadcasted_iota(jnp.int32, (ch, ch), 0)
    b = lax.broadcasted_iota(jnp.int32, (ch, ch), 1)
    group_of = lambda i: lax.shift_right_logical(i * 43691, 19)
    ind[...] = jnp.where(group_of(a) == group_of(b), 1.0, 0.0).astype(BF16)

    def over_group(v):
        v = jnp.broadcast_to(v, (8, ch))
        hi = v.astype(BF16).astype(F32)
        mid = (v - hi).astype(BF16).astype(F32)
        lo = v - hi - mid
        parts = jnp.concatenate([hi, mid, lo, jnp.zeros_like(v)], axis=0).astype(BF16)
        got = jnp.dot(parts, ind[...], preferred_element_type=F32)
        return got[0:1] + (got[8:9] + got[16:17])

    load.wait()
    pixels = 1.0 * frames * height * width

    def fold(v):
        return jnp.sum(v.reshape(-1, 32, ch), axis=0)

    def over_rows(v):
        return jnp.sum(v, axis=0, keepdims=True)

    pivot = over_rows(fold(xo[0, 1].astype(F32))) * (1.0 / width)

    def sums(i, acc):
        first, second = acc
        d = xo[lax.div(i, height), 1 + lax.rem(i, height)].astype(F32) - pivot
        return first + fold(d), second + fold(d * d)

    zero = jnp.zeros((32, ch), F32)
    first, second = lax.fori_loop(0, frames * height, sums, (zero, zero))
    first, second = over_rows(first), over_rows(second)
    mean = pivot + first * (1.0 / pixels)
    square = second - first * (first * (1.0 / pixels))

    top = lax.broadcasted_iota(jnp.int32, (2, ch), 0) == 0

    def exchange(mean, square, count, peers, outbox, inbox, ssem, rsem, between):
        size = len(peers) + 1
        outbox[...] = jnp.where(top, mean, square)
        copies = [
            pltpu.make_async_remote_copy(
                src_ref=outbox, dst_ref=inbox.at[d], send_sem=ssem.at[d], recv_sem=rsem.at[d],
                device_id=peers[d], device_id_type=MESH,
            )
            for d in range(size - 1)
        ]
        for c in copies:
            c.start()
        between()
        for c in copies:
            c.wait()
        got = [inbox[d] for d in range(size - 1)]
        means = [mean] + [g[0:1] for g in got]
        whole = sum(means) * (1.0 / size)
        squares = square + sum(g[1:2] for g in got)
        for m in means:
            squares = squares + count * ((m - whole) * (m - whole))
        return whole, squares

    def frames_away():
        @pl.when(sends_on)
        def _():
            back(0).start()
            for i in range(len(PIECES)):
                bulk(i).start()

    def edges_away():
        @pl.when(up_on)
        def _():
            own_edge(0).start()

        @pl.when(down_on)
        def _():
            own_edge(1).start()

    pl.semaphore_wait(barrier, len(tm_peers) + len(row_peers))
    mean, square = exchange(
        mean, square, pixels, tm_peers, tm_out, tm_in, tm_send, tm_recv, frames_away
    )
    mean, square = exchange(
        mean, square, pixels * n_tm, row_peers, row_out, row_in, row_send, row_recv, edges_away
    )
    channel_mean = mean
    mean = over_group(channel_mean) * (1.0 / per_group)
    off = channel_mean - mean
    square = over_group(square + (pixels * n_tm * n_rows) * (off * off))
    inverse = lax.rsqrt(square * (1.0 / cells) + EPS)
    vector.wait()
    scale = 0.5 * (inverse * gv[pl.ds(0, ch)].reshape(1, ch))
    shift = 0.5 * gv[pl.ds(ch, ch)].reshape(1, ch)

    def normalize(src, f, dst, row):
        h = (src[f, row].astype(F32) - mean) * scale + shift
        h = h + h * jnp.tanh(h)
        if row == 0:
            h = jnp.where(up_on, h, 0.0)
        if row == height + 1:
            h = jnp.where(down_on, h, 0.0)
        dst[row] = h.astype(BF16)

    def norms(src, f, dst, rows):
        return [functools.partial(normalize, src, f, dst, row) for row in rows]

    cut = 4 * 256

    def lhs_of(used, first, rows):
        return jnp.concatenate(
            [
                act[pl.ds(first + kh, rows)].reshape(rows * width, ch)
                for act in used
                for kh in range(3)
            ],
            axis=1,
        )

    def put(t, first, rows, lo, got, add):
        got = got.reshape(rows, width, got.shape[1])
        at = (t, pl.ds(first, rows), slice(None), pl.ds(lo, got.shape[2]))
        z[at] = z[at] + got if add else got

    def weights(kt, n, lo, size):
        return wv[pl.ds(kt, n), :, :, pl.ds(lo, size)].reshape(n * 3 * ch, size)

    def main(t, used, kt, first, rows, add):
        def tile(lo):
            got = jnp.dot(
                lhs_of(used, first, rows), weights(kt, len(used), lo, 256), preferred_element_type=F32
            )
            put(t, first, rows, lo, got, add)

        return [functools.partial(tile, lo) for lo in range(0, cut, 256)]

    def pair(act, kts, first, rows, add):
        def tile():
            rhs = jnp.concatenate([weights(kt, 1, cut, 128) for kt in kts], axis=1)
            got = jnp.dot(lhs_of((act,), first, rows), rhs, preferred_element_type=F32)
            put(0, first, rows, cut, got[:, :128], add)
            put(1, first, rows, cut, got[:, 128:], add)

        return [tile]

    def single(t, act, kt, first, rows):
        def tile():
            got = jnp.dot(
                lhs_of((act,), first, rows), weights(kt, 1, cut, 128), preferred_element_type=F32
            )
            put(t, first, rows, cut, got, True)

        return [tile]

    def run(tiles, side=()):
        done = 0
        for i, tile in enumerate(tiles):
            tile()
            upto = len(side) * (i + 1) // len(tiles)
            for task in side[done:upto]:
                task()
            done = upto

    wi = lax.broadcasted_iota(jnp.int32, (width, ch), 0)

    def finish(t, h):
        left = pltpu.roll(z[t, h, :, 0:ch], 1, 0)
        right = pltpu.roll(z[t, h, :, 2 * ch : 3 * ch], width - 1, 0)
        conv = z[t, h, :, ch : 2 * ch]
        conv = conv + jnp.where(wi == 0, 0.0, left) + jnp.where(wi == width - 1, 0.0, right)
        cbias = gv[pl.ds(2 * ch, ch)].reshape(1, ch)
        out[0, t, h] = (xo[t, h + 1].astype(F32) + conv + cbias).astype(BF16)

    def finishes(t, first, rows):
        return [functools.partial(finish, t, h) for h in range(first, first + rows)]

    def forward(f):
        @pl.when(recvs_on)
        def _():
            a, b = [i for i, p in enumerate(PIECES) if p[0] == f][:2]
            bulk(a).wait_recv()
            bulk(b).wait_recv()

            @pl.when(up_on)
            def _():
                fwd_edge(f, 0).start()

            @pl.when(down_on)
            def _():
                fwd_edge(f, 1).start()

    def edge_in(f, i):
        @pl.when(down_on if i == 0 else up_on)
        def _():
            fwd_edge(f, i).wait_recv()

    @pl.when(down_on)
    def _():
        own_edge(0).wait_recv()

    @pl.when(up_on)
    def _():
        own_edge(1).wait_recv()

    low, high = range(0, half + 2), range(half + 2, height + 2)
    for task in norms(xo, 0, act_c, low):
        task()
    for c in wloads:
        c.wait()

    def own(first, side0, side1):
        run(
            main(0, (act_c,), 2, first, half, False) + pair(act_c, (2, 1), first, half, False), side0
        )
        forwards[first]()
        run(
            main(1, (act_c, act_d), 1, first, half, False) + single(1, act_d, 2, first, half), side1
        )

    def after_first():
        @pl.when(second_on)
        def _():
            back(0).wait_recv()
            back(1).start()

        forward(1)

    def before_last():
        @pl.when(recvs_on)
        def _():
            edge_in(1, 1)
            bulk(2).wait_recv()

    forwards = {0: after_first, half: before_last}
    own(0, norms(xo, 1, act_d, low), norms(xo, 0, act_c, high) + norms(xo, 1, act_d, high))
    own(half, (), norms(xr, 1, act_b, low))

    @pl.when(third_on)
    def _():
        back(1).wait_recv()
        back(2).start()

    @pl.when(recvs_on)
    def _():
        run(main(0, (act_b,), 1, 0, half, True))
        edge_in(1, 0)
        bulk(3).wait_recv()
        run(
            main(1, (act_b,), 0, 0, half, True) + pair(act_b, (1, 0), 0, half, True),
            norms(xr, 1, act_b, high),
        )
        run(
            main(0, (act_b,), 1, half, half, True)
            + main(1, (act_b,), 0, half, half, True)
            + pair(act_b, (1, 0), half, half, True),
            finishes(1, 0, half),
        )

    forward(0)

    @pl.when(recvs_on)
    def _():
        for task in finishes(1, half, half):
            task()
        bulk(6).wait_recv()
        for task in norms(xr, 0, act_a, (1, 2, 3, 8)):
            task()
        edge_in(0, 0)
        edge_in(0, 1)
        for task in norms(xr, 0, act_a, (0, 9)):
            task()
        back(2).wait_recv()
        for task in norms(xr, 0, act_a, (4, 5, 6)):
            task()
        run(main(0, (act_a,), 0, 0, half, True) + single(0, act_a, 0, 0, half))
        bulk(7).wait_recv()
        for task in norms(xr, 0, act_a, (7,)):
            task()
        run(
            main(0, (act_a,), 0, half, half, True) + single(0, act_a, 0, half, half),
            finishes(0, 0, half),
        )
        for task in finishes(0, half, half):
            task()

    @pl.when(jnp.logical_not(recvs_on))
    def _():
        for t in range(frames):
            for task in finishes(t, 0, height):
                task()

    @pl.when(sends_on)
    def _():
        for i in range(len(PIECES)):
            bulk(i).wait_send()
        back(0).wait_send()

    @pl.when(second_on)
    def _():
        back(1).wait_send()

    @pl.when(third_on)
    def _():
        back(2).wait_send()

    for i, on in ((0, up_on), (1, down_on)):

        @pl.when(on)
        def _():
            own_edge(i).wait_send()

            @pl.when(recvs_on)
            def _():
                for f in range(2):
                    fwd_edge(f, i).wait_send()


def shards(inputs, norm_gain, norm_bias, conv_weight, conv_bias):
    clips, frames, height, width, ch = inputs.shape
    n_tm, n_rows = lax.axis_size("tm"), lax.axis_size("rows")
    per_group = ch // GROUPS
    cells = 1.0 * clips * frames * height * width * per_group * n_tm * n_rows
    hbm = pl.BlockSpec(memory_space=pltpu.HBM)
    dma = lambda n: pltpu.SemaphoreType.DMA((n,))
    act = pltpu.VMEM((height + 2, width, ch), BF16)
    hop = pltpu.VMEM((BACK[1], width, ch), BF16)
    return pl.pallas_call(
        functools.partial(kernel, cells, per_group),
        out_shape=jax.ShapeDtypeStruct(inputs.shape, BF16),
        in_specs=[hbm] * 3,
        out_specs=pl.BlockSpec(memory_space=pltpu.VMEM),
        scratch_shapes=[
            pltpu.VMEM((frames, height + 2, width, ch), BF16),
            pltpu.VMEM((2, height + 2, width, ch), BF16),
            act,
            act,
            act,
            act,
            pltpu.VMEM((3, 3, ch, 3 * ch), BF16),
            pltpu.VMEM((frames, height, width, 3 * ch), F32),
            pltpu.VMEM((ch, ch), BF16),
            pltpu.VMEM((2, ch), F32),
            pltpu.VMEM((n_tm - 1, 2, ch), F32),
            pltpu.VMEM((2, ch), F32),
            pltpu.VMEM((n_rows - 1, 2, ch), F32),
            hop,
            hop,
            pltpu.VMEM((3 * ch,), F32),
            pltpu.SemaphoreType.DMA,
            dma(3),
            pltpu.SemaphoreType.DMA,
            dma(len(PIECES)),
            dma(len(PIECES)),
            dma(3),
            dma(3),
            dma(2),
            dma(2),
            dma(4),
            dma(4),
            dma(n_tm - 1),
            dma(n_tm - 1),
            dma(n_rows - 1),
            dma(n_rows - 1),
        ],
        compiler_params=pltpu.CompilerParams(
            collective_id=0, has_side_effects=True, vmem_limit_bytes=51 * 1024 * 1024
        ),
    )(inputs, jnp.concatenate([norm_gain, norm_bias, conv_bias]), conv_weight)


def solution(mesh):
    placed = (P("batch", "tm", "rows", None, None), P(), P(), P(), P())
    return jax.shard_map(
        shards,
        mesh=mesh,
        in_specs=placed,
        out_specs=P("batch", "tm", "rows", None, None),
        check_vma=False,
    )
```

time: 44.2 us -> 40 us (0.905)
  Pallas kernels: 41.7 us -> 37.8 us
    pallas_call x1, Pallas kernels: 41.7 us -> 37.8 us  [shards(): pl.pallas_call(functools.partial(kernel, cells, per_group), out_shape=jax...]
where the time goes in v3:
time: 40 us; the launch traced here: 39.7 us
  Pallas kernels  37.8 us (94%)
  local copies, waits for them, and re-layouts  1.15 us (3%)
  other arithmetic  0.72 us (2%)
    pallas_call x1, Pallas kernels, shards(): pl.pallas_call(functools.partial(kernel, cells, per_group), out_shape=jax...  37.8 us
    unnamed x1, local copies, waits for them, and re-layouts  1.15 us

profile of v3, /device:TPU:99, one launch (start us, length us, event | category | flops | bytes accessed | tf_op | source)
XLA Modules:
  0.0 39.7 jit_solution(15122710654151350023)
XLA Ops:
  0.0 0.7 %pad_maximum_fusion.vec = f32[1152]{0:T(1024)S(1)} fusion(f32[384]{0:T(512)} %param.9, f32[384]{0:T(512)} %param.7, f32[384]{0:T(512)} %param.6), kind=kLoop, calls=%fused_computation | loop fusion | flops 2304 | bytes 9216 | tf_op jit(solution)/shard_map/concatenate | solution.py:472
  0.7 37.8 %shard_map.55 = bf16[1,2,8,128,384]{4,3,2,1,0:T(8,128)(2,1)S(1)} custom-call(bf16[1,2,8,128,384]{4,3,2,1,0:T(8,128)(2,1)} %x.1, f32[1152]{0:T(1024)S(1)} %pad_maximum_fusion.vec, bf16[3,3,3,384,384]{4,3,2,1,0:T(8,128)(2,1)} %w.1), custom_call_target="tpu_custom_call" | custom-call | tf_op jit(solution)/shard_map/pallas_call | solution.py:431
  38.6 1.1 %copy.7 = bf16[1,2,8,128,384]{4,3,2,1,0:T(8,128)(2,1)} copy(bf16[1,2,8,128,384]{4,3,2,1,0:T(8,128)(2,1)S(1)} %shard_map.55) | data formatting | bytes 3145728

commit v4 on v3

--- a/solution.py
+++ b/solution.py
@@ -13,8 +13,8 @@
 F32 = jnp.float32
 BF16 = jnp.bfloat16
 
-PIECES = ((1, 0, 1), (1, 7, 1), (1, 1, 4), (1, 5, 2), (0, 0, 1), (0, 7, 1), (0, 1, 2), (0, 6, 1))
-BACK = (3, 3)
+PIECES = ((1, 0, 1), (1, 7, 1), (1, 1, 4), (1, 5, 2), (0, 0, 1), (0, 7, 1), (0, 3, 2))
+BACK = ((1, 2), (5, 2))
 
 
 def kernel(
@@ -50,7 +50,7 @@
     def bulk(i):
         f, first, rows = PIECES[i]
         return pltpu.make_async_remote_copy(
-            src_ref=x.at[0, f, pl.ds(first, rows)],
+            src_ref=xo.at[f, pl.ds(1 + first, rows)],
             dst_ref=xr.at[f, pl.ds(1 + first, rows)],
             send_sem=bulk_send.at[i],
             recv_sem=bulk_recv.at[i],
@@ -58,17 +58,19 @@
             device_id_type=MESH,
         )
 
-    def back(i):
-        first, rows = BACK
-        src, dst = (
-            (x.at[0, 0, pl.ds(first, rows)], hop1),
-            (hop1, hop2),
-            (hop2, xr.at[0, pl.ds(1 + first, rows)]),
-        )[i]
+    def back(hop, p):
+        first, rows = BACK[p]
+        mine, place = xo.at[0, pl.ds(1 + first, rows)], xr.at[0, pl.ds(1 + first, rows)]
+        line = (mine, hop1.at[p, pl.ds(0, rows)], hop2.at[p, pl.ds(0, rows)], place)
         return pltpu.make_async_remote_copy(
-            src_ref=src, dst_ref=dst, send_sem=back_send.at[i], recv_sem=back_recv.at[i],
+            src_ref=line[hop], dst_ref=line[hop + 1],
+            send_sem=back_send.at[len(BACK) * hop + p], recv_sem=back_recv.at[len(BACK) * hop + p],
             device_id={"tm": lax.rem(j + n_tm - 1, n_tm)}, device_id_type=MESH,
         )
+
+    def pass_back(hop, p):
+        back(hop - 1, p).wait_recv()
+        back(hop, p).start()
 
     def edge(i, src, dst, ssem, rsem):
         return pltpu.make_async_remote_copy(
@@ -79,7 +81,7 @@
 
     def own_edge(i):
         return edge(
-            i, x.at[0, :, 0 if i == 0 else height - 1], xo.at[:, height + 1 if i == 0 else 0],
+            i, xo.at[:, 1 if i == 0 else height], xo.at[:, height + 1 if i == 0 else 0],
             halo_send.at[i], halo_recv.at[i],
         )
 
@@ -89,20 +91,7 @@
             fwd_send.at[2 * f + i], fwd_recv.at[2 * f + i],
         )
 
-    sends_on, recvs_on = j < n_tm - 1, j > 0
-    second_on, third_on = j != n_tm - 2, j != n_tm - 3
-    up_on, down_on = r > 0, r < n_rows - 1
-
-    @pl.when(jnp.logical_not(recvs_on))
-    def _():
-        xr[...] = jnp.zeros_like(xr)
-
-    for on, row in ((up_on, 0), (down_on, height + 1)):
-
-        @pl.when(jnp.logical_not(on))
-        def _():
-            xo[:, row] = jnp.zeros((frames, width, ch), BF16)
-            xr[:, row] = jnp.zeros((2, width, ch), BF16)
+    recvs_on, up_on, down_on = j > 0, r > 0, r < n_rows - 1
 
     a = lax.broadcasted_iota(jnp.int32, (ch, ch), 0)
     b = lax.broadcasted_iota(jnp.int32, (ch, ch), 1)
@@ -166,28 +155,21 @@
         return whole, squares
 
     def frames_away():
-        @pl.when(sends_on)
-        def _():
-            back(0).start()
-            for i in range(len(PIECES)):
-                bulk(i).start()
-
-    def edges_away():
-        @pl.when(up_on)
-        def _():
-            own_edge(0).start()
-
-        @pl.when(down_on)
-        def _():
-            own_edge(1).start()
+        for p in range(len(BACK)):
+            back(0, p).start()
+        for i in range(len(PIECES)):
+            bulk(i).start()
+        own_edge(0).start()
+        own_edge(1).start()
 
     pl.semaphore_wait(barrier, len(tm_peers) + len(row_peers))
     mean, square = exchange(
         mean, square, pixels, tm_peers, tm_out, tm_in, tm_send, tm_recv, frames_away
     )
     mean, square = exchange(
-        mean, square, pixels * n_tm, row_peers, row_out, row_in, row_send, row_recv, edges_away
-    )
+        mean, square, pixels * n_tm, row_peers, row_out, row_in, row_send, row_recv, lambda: None
+    )
+    pass_back(1, 0)
     channel_mean = mean
     mean = over_group(channel_mean) * (1.0 / per_group)
     off = channel_mean - mean
@@ -197,14 +179,15 @@
     scale = 0.5 * (inverse * gv[pl.ds(0, ch)].reshape(1, ch))
     shift = 0.5 * gv[pl.ds(ch, ch)].reshape(1, ch)
 
+    def kept(on):
+        return jnp.where(on, scale, 0.0), jnp.where(on, shift, 0.0)
+
+    factors = [kept(up_on), (scale, shift), kept(down_on)]
+
     def normalize(src, f, dst, row):
-        h = (src[f, row].astype(F32) - mean) * scale + shift
-        h = h + h * jnp.tanh(h)
-        if row == 0:
-            h = jnp.where(up_on, h, 0.0)
-        if row == height + 1:
-            h = jnp.where(down_on, h, 0.0)
-        dst[row] = h.astype(BF16)
+        by, plus = factors[0 if row == 0 else 2 if row == height + 1 else 1]
+        h = (src[f, row].astype(F32) - mean) * by + plus
+        dst[row] = (h + h * jnp.tanh(h)).astype(BF16)
 
     def norms(src, f, dst, rows):
         return [functools.partial(normalize, src, f, dst, row) for row in rows]
@@ -279,144 +262,96 @@
         return [functools.partial(finish, t, h) for h in range(first, first + rows)]
 
     def forward(f):
-        @pl.when(recvs_on)
-        def _():
-            a, b = [i for i, p in enumerate(PIECES) if p[0] == f][:2]
-            bulk(a).wait_recv()
-            bulk(b).wait_recv()
-
-            @pl.when(up_on)
-            def _():
-                fwd_edge(f, 0).start()
-
-            @pl.when(down_on)
-            def _():
-                fwd_edge(f, 1).start()
-
-    def edge_in(f, i):
-        @pl.when(down_on if i == 0 else up_on)
-        def _():
-            fwd_edge(f, i).wait_recv()
-
-    @pl.when(down_on)
-    def _():
-        own_edge(0).wait_recv()
-
-    @pl.when(up_on)
-    def _():
-        own_edge(1).wait_recv()
+        for i, p in enumerate(PIECES):
+            if p in ((f, 0, 1), (f, height - 1, 1)):
+                bulk(i).wait_recv()
+        fwd_edge(f, 0).start()
+        fwd_edge(f, 1).start()
+
+    def edges_in(f):
+        fwd_edge(f, 0).wait_recv()
+        fwd_edge(f, 1).wait_recv()
 
     low, high = range(0, half + 2), range(half + 2, height + 2)
-    for task in norms(xo, 0, act_c, low):
-        task()
+    forward(1)
+    own_edge(0).wait_recv()
+    own_edge(1).wait_recv()
+
+    run(norms(xo, 0, act_c, low))
     for c in wloads:
         c.wait()
-
-    def own(first, side0, side1):
-        run(
-            main(0, (act_c,), 2, first, half, False) + pair(act_c, (2, 1), first, half, False), side0
-        )
-        forwards[first]()
-        run(
-            main(1, (act_c, act_d), 1, first, half, False) + single(1, act_d, 2, first, half), side1
-        )
-
-    def after_first():
-        @pl.when(second_on)
-        def _():
-            back(0).wait_recv()
-            back(1).start()
-
-        forward(1)
-
-    def before_last():
-        @pl.when(recvs_on)
-        def _():
-            edge_in(1, 1)
-            bulk(2).wait_recv()
-
-    forwards = {0: after_first, half: before_last}
-    own(0, norms(xo, 1, act_d, low), norms(xo, 0, act_c, high) + norms(xo, 1, act_d, high))
-    own(half, (), norms(xr, 1, act_b, low))
-
-    @pl.when(third_on)
-    def _():
-        back(1).wait_recv()
-        back(2).start()
+    run(
+        main(0, (act_c,), 2, 0, half, False) + pair(act_c, (2, 1), 0, half, False),
+        norms(xo, 1, act_d, low),
+    )
+    run(
+        main(1, (act_c, act_d), 1, 0, half, False) + single(1, act_d, 2, 0, half),
+        norms(xo, 0, act_c, high) + norms(xo, 1, act_d, high),
+    )
+    pass_back(1, 1)
+    run(main(0, (act_c,), 2, half, half, False) + pair(act_c, (2, 1), half, half, False))
+    pass_back(2, 0)
+    edges_in(1)
+    bulk(2).wait_recv()
+    run(
+        main(1, (act_c, act_d), 1, half, half, False) + single(1, act_d, 2, half, half),
+        norms(xr, 1, act_b, low),
+    )
+    pass_back(2, 1)
+    bulk(3).wait_recv()
 
     @pl.when(recvs_on)
     def _():
-        run(main(0, (act_b,), 1, 0, half, True))
-        edge_in(1, 0)
-        bulk(3).wait_recv()
         run(
-            main(1, (act_b,), 0, 0, half, True) + pair(act_b, (1, 0), 0, half, True),
+            main(0, (act_b,), 1, 0, half, True)
+            + main(1, (act_b,), 0, 0, half, True)
+            + pair(act_b, (1, 0), 0, half, True),
             norms(xr, 1, act_b, high),
         )
+        forward(0)
+        back(2, 0).wait_recv()
         run(
             main(0, (act_b,), 1, half, half, True)
             + main(1, (act_b,), 0, half, half, True)
             + pair(act_b, (1, 0), half, half, True),
-            finishes(1, 0, half),
-        )
-
-    forward(0)
-
-    @pl.when(recvs_on)
-    def _():
-        for task in finishes(1, half, half):
-            task()
+            norms(xr, 0, act_a, (1, 2, 3, 8)) + finishes(1, 0, half),
+        )
         bulk(6).wait_recv()
-        for task in norms(xr, 0, act_a, (1, 2, 3, 8)):
-            task()
-        edge_in(0, 0)
-        edge_in(0, 1)
-        for task in norms(xr, 0, act_a, (0, 9)):
-            task()
-        back(2).wait_recv()
-        for task in norms(xr, 0, act_a, (4, 5, 6)):
-            task()
-        run(main(0, (act_a,), 0, 0, half, True) + single(0, act_a, 0, 0, half))
-        bulk(7).wait_recv()
-        for task in norms(xr, 0, act_a, (7,)):
-            task()
+        back(2, 1).wait_recv()
+        edges_in(0)
+        run(norms(xr, 0, act_a, (0, 4, 5)))
         run(
-            main(0, (act_a,), 0, half, half, True) + single(0, act_a, 0, half, half),
-            finishes(0, 0, half),
-        )
-        for task in finishes(0, half, half):
-            task()
+            main(0, (act_a,), 0, 0, half, True) + single(0, act_a, 0, 0, half),
+            norms(xr, 0, act_a, (6, 7, 9)) + finishes(1, half, half),
+        )
+        run(
+            main(0, (act_a,), 0, half, 2, True) + single(0, act_a, 0, half, 2), finishes(0, 0, half)
+        )
+        run(
+            main(0, (act_a,), 0, half + 2, 2, True) + single(0, act_a, 0, half + 2, 2),
+            finishes(0, half, 2),
+        )
+        run(finishes(0, half + 2, 2))
 
     @pl.when(jnp.logical_not(recvs_on))
     def _():
         for t in range(frames):
-            for task in finishes(t, 0, height):
-                task()
-
-    @pl.when(sends_on)
-    def _():
-        for i in range(len(PIECES)):
-            bulk(i).wait_send()
-        back(0).wait_send()
-
-    @pl.when(second_on)
-    def _():
-        back(1).wait_send()
-
-    @pl.when(third_on)
-    def _():
-        back(2).wait_send()
-
-    for i, on in ((0, up_on), (1, down_on)):
-
-        @pl.when(on)
-        def _():
-            own_edge(i).wait_send()
-
-            @pl.when(recvs_on)
-            def _():
-                for f in range(2):
-                    fwd_edge(f, i).wait_send()
+            run(finishes(t, 0, height))
+        forward(0)
+        edges_in(0)
+        bulk(6).wait_recv()
+        for p in range(len(BACK)):
+            back(2, p).wait_recv()
+
+    for i in range(len(PIECES)):
+        bulk(i).wait_send()
+    for hop in range(3):
+        for p in range(len(BACK)):
+            back(hop, p).wait_send()
+    for i in range(2):
+        own_edge(i).wait_send()
+        for f in range(2):
+            fwd_edge(f, i).wait_send()
 
 
 def shards(inputs, norm_gain, norm_bias, conv_weight, conv_bias):
@@ -427,7 +362,7 @@
     hbm = pl.BlockSpec(memory_space=pltpu.HBM)
     dma = lambda n: pltpu.SemaphoreType.DMA((n,))
     act = pltpu.VMEM((height + 2, width, ch), BF16)
-    hop = pltpu.VMEM((BACK[1], width, ch), BF16)
+    hop = pltpu.VMEM((len(BACK), BACK[0][1], width, ch), BF16)
     return pl.pallas_call(
         functools.partial(kernel, cells, per_group),
         out_shape=jax.ShapeDtypeStruct(inputs.shape, BF16),
@@ -455,8 +390,8 @@
             pltpu.SemaphoreType.DMA,
             dma(len(PIECES)),
             dma(len(PIECES)),
-            dma(3),
-            dma(3),
+            dma(3 * len(BACK)),
+            dma(3 * len(BACK)),
             dma(2),
             dma(2),
             dma(4),

time: 40 us -> 38.4 us (0.960)
  the two profiles are of different devices: /device:TPU:99 before, /device:TPU:6 now
where the time goes in v4:
time: 38.4 us; the launch traced here: 38.2 us
  Pallas kernels  36.4 us (95%)
  local copies, waits for them, and re-layouts  1.15 us (3%)
  other arithmetic  0.72 us (2%)
    pallas_call x1, Pallas kernels, shards(): pl.pallas_call(functools.partial(kernel, cells, per_group), out_shape=jax...  36.4 us
    unnamed x1, local copies, waits for them, and re-layouts  1.15 us

profile of v4, /device:TPU:6, one launch (start us, length us, event | category | flops | bytes accessed | tf_op | source)
XLA Modules:
  0.0 38.2 jit_solution(17586868387926177645)
XLA Ops:
  0.0 0.7 %pad_maximum_fusion.vec = f32[1152]{0:T(1024)S(1)} fusion(f32[384]{0:T(512)} %param.9, f32[384]{0:T(512)} %param.7, f32[384]{0:T(512)} %param.6), kind=kLoop, calls=%fused_computation | loop fusion | flops 2304 | bytes 9216 | tf_op jit(solution)/shard_map/concatenate | solution.py:407
  0.7 36.4 %shard_map.55 = bf16[1,2,8,128,384]{4,3,2,1,0:T(8,128)(2,1)S(1)} custom-call(bf16[1,2,8,128,384]{4,3,2,1,0:T(8,128)(2,1)} %x.1, f32[1152]{0:T(1024)S(1)} %pad_maximum_fusion.vec, bf16[3,3,3,384,384]{4,3,2,1,0:T(8,128)(2,1)} %w.1), custom_call_target="tpu_custom_call" | custom-call | tf_op jit(solution)/shard_map/pallas_call | solution.py:366
  37.1 1.1 %copy.7 = bf16[1,2,8,128,384]{4,3,2,1,0:T(8,128)(2,1)} copy(bf16[1,2,8,128,384]{4,3,2,1,0:T(8,128)(2,1)S(1)} %shard_map.55) | data formatting | bytes 3145728

commit v5 on v4

--- a/solution.py
+++ b/solution.py
@@ -13,7 +13,7 @@
 F32 = jnp.float32
 BF16 = jnp.bfloat16
 
-PIECES = ((1, 0, 1), (1, 7, 1), (1, 1, 4), (1, 5, 2), (0, 0, 1), (0, 7, 1), (0, 3, 2))
+PIECES = ((1, 0, 1), (1, 7, 1), (1, 1, 4), (1, 5, 2), (0, 0, 1), (0, 7, 1), (0, 3, 1), (0, 4, 1))
 BACK = ((1, 2), (5, 2))
 
 
@@ -239,6 +239,17 @@
 
         return [tile]
 
+    def some(first, rows, khs):
+        def tile(lo):
+            n = min(256, 3 * ch - lo)
+            lhs = jnp.concatenate(
+                [act_a[pl.ds(first + kh, rows)].reshape(rows * width, ch) for kh in khs], axis=1
+            )
+            rhs = jnp.concatenate([wv[0, kh, :, pl.ds(lo, n)] for kh in khs], axis=0)
+            put(0, first, rows, lo, jnp.dot(lhs, rhs, preferred_element_type=F32), True)
+
+        return [functools.partial(tile, lo) for lo in range(0, 3 * ch, 256)]
+
     def run(tiles, side=()):
         done = 0
         for i, tile in enumerate(tiles):
@@ -289,57 +300,65 @@
         norms(xo, 0, act_c, high) + norms(xo, 1, act_d, high),
     )
     pass_back(1, 1)
-    run(main(0, (act_c,), 2, half, half, False) + pair(act_c, (2, 1), half, half, False))
+    edges_in(1)
+    run(
+        pair(act_c, (2, 1), half, half, False)
+        + main(1, (act_c, act_d), 1, half, half, False)
+        + single(1, act_d, 2, half, half),
+        norms(xr, 1, act_b, (0, 1, 8, 9)),
+    )
     pass_back(2, 0)
-    edges_in(1)
-    bulk(2).wait_recv()
-    run(
-        main(1, (act_c, act_d), 1, half, half, False) + single(1, act_d, 2, half, half),
-        norms(xr, 1, act_b, low),
-    )
-    pass_back(2, 1)
-    bulk(3).wait_recv()
 
     @pl.when(recvs_on)
     def _():
+        bulk(2).wait_recv()
+        run(norms(xr, 1, act_b, (2, 3, 4, 5)))
         run(
             main(0, (act_b,), 1, 0, half, True)
             + main(1, (act_b,), 0, 0, half, True)
-            + pair(act_b, (1, 0), 0, half, True),
-            norms(xr, 1, act_b, high),
+            + pair(act_b, (1, 0), 0, half, True)
+        )
+        pass_back(2, 1)
+        bulk(3).wait_recv()
+        run(norms(xr, 1, act_b, (6, 7)))
+        run(
+            main(0, (act_b, act_c), 1, half, half, False) + main(1, (act_b,), 0, half, half, True),
+            finishes(1, 0, half),
         )
         forward(0)
         back(2, 0).wait_recv()
+        run(pair(act_b, (1, 0), half, half, True), norms(xr, 0, act_a, (1, 2, 3)))
         run(
-            main(0, (act_b,), 1, half, half, True)
-            + main(1, (act_b,), 0, half, half, True)
-            + pair(act_b, (1, 0), half, half, True),
-            norms(xr, 0, act_a, (1, 2, 3, 8)) + finishes(1, 0, half),
+            some(1, 1, (0, 1, 2)) + some(0, 1, (1, 2)) + some(2, 1, (0, 1)) + some(3, 1, (0,)),
+            norms(xr, 0, act_a, (8,)) + finishes(1, half, half),
         )
         bulk(6).wait_recv()
+        run(norms(xr, 0, act_a, (4,)))
+        run(
+            some(3, 1, (1,)) + some(2, 1, (2,)) + some(4, 1, (0,)) + some(6, 1, (2,)) + some(7, 1, (1,)),
+            finishes(0, 1, 2),
+        )
+        bulk(7).wait_recv()
         back(2, 1).wait_recv()
         edges_in(0)
-        run(norms(xr, 0, act_a, (0, 4, 5)))
-        run(
-            main(0, (act_a,), 0, 0, half, True) + single(0, act_a, 0, 0, half),
-            norms(xr, 0, act_a, (6, 7, 9)) + finishes(1, half, half),
-        )
-        run(
-            main(0, (act_a,), 0, half, 2, True) + single(0, act_a, 0, half, 2), finishes(0, 0, half)
-        )
-        run(
-            main(0, (act_a,), 0, half + 2, 2, True) + single(0, act_a, 0, half + 2, 2),
-            finishes(0, half, 2),
-        )
-        run(finishes(0, half + 2, 2))
+        run(norms(xr, 0, act_a, (5, 0)))
+        run(some(3, 1, (2,)) + some(0, 1, (0,)), norms(xr, 0, act_a, (6, 7, 9)))
+        run(some(4, 1, (1, 2)), finishes(0, 0, 1))
+        run(some(5, 1, (0, 1, 2)), finishes(0, 3, 2))
+        run(some(6, 1, (0, 1)), finishes(0, 5, 1))
+        run(some(7, 1, (0, 2)), finishes(0, 6, 1))
+        run(finishes(0, 7, 1))
 
     @pl.when(jnp.logical_not(recvs_on))
     def _():
+        run(main(0, (act_c,), 2, half, half, False))
+        pass_back(2, 1)
         for t in range(frames):
             run(finishes(t, 0, height))
         forward(0)
         edges_in(0)
-        bulk(6).wait_recv()
+        for i in (2, 3, 6, 7):
+            bulk(i).wait_recv()
         for p in range(len(BACK)):
             back(2, p).wait_recv()
 

time: 38.4 us -> 35.9 us (0.935)
  the two profiles are of different devices: /device:TPU:6 before, /device:TPU:99 now
where the time goes in v5:
time: 35.9 us; the launch traced here: 35.7 us
  Pallas kernels  33.8 us (94%)
  local copies, waits for them, and re-layouts  1.15 us (3%)
  other arithmetic  0.72 us (2%)
    pallas_call x1, Pallas kernels, shards(): pl.pallas_call(functools.partial(kernel, cells, per_group), out_shape=jax...  33.8 us
    unnamed x1, local copies, waits for them, and re-layouts  1.15 us
    concatenate x1, other arithmetic, shards(): jnp.concatenate([norm_gain, norm_bias, conv_bias])  0.72 us

profile of v5, /device:TPU:99, one launch (start us, length us, event | category | flops | bytes accessed | tf_op | source)
XLA Modules:
  0.0 35.7 jit_solution(7444120719021764918)
XLA Ops:
  0.0 0.7 %pad_maximum_fusion.vec = f32[1152]{0:T(1024)S(1)} fusion(f32[384]{0:T(512)} %param.9, f32[384]{0:T(512)} %param.7, f32[384]{0:T(512)} %param.6), kind=kLoop, calls=%fused_computation | loop fusion | flops 2304 | bytes 9216 | tf_op jit(solution)/shard_map/concatenate | solution.py:426
  0.7 33.8 %shard_map.55 = bf16[1,2,8,128,384]{4,3,2,1,0:T(8,128)(2,1)S(1)} custom-call(bf16[1,2,8,128,384]{4,3,2,1,0:T(8,128)(2,1)} %x.1, f32[1152]{0:T(1024)S(1)} %pad_maximum_fusion.vec, bf16[3,3,3,384,384]{4,3,2,1,0:T(8,128)(2,1)} %w.1), custom_call_target="tpu_custom_call" | custom-call | tf_op jit(solution)/shard_map/pallas_call | solution.py:385
  34.5 1.1 %copy.7 = bf16[1,2,8,128,384]{4,3,2,1,0:T(8,128)(2,1)} copy(bf16[1,2,8,128,384]{4,3,2,1,0:T(8,128)(2,1)S(1)} %shard_map.55) | data formatting | bytes 3145728

commit v6 on v5

--- a/solution.py
+++ b/solution.py
@@ -13,13 +13,13 @@
 F32 = jnp.float32
 BF16 = jnp.bfloat16
 
-PIECES = ((1, 0, 1), (1, 7, 1), (1, 1, 4), (1, 5, 2), (0, 0, 1), (0, 7, 1), (0, 3, 1), (0, 4, 1))
-BACK = ((1, 2), (5, 2))
+PIECES = ((1, 0, 1), (1, 7, 1), (1, 1, 4), (1, 5, 2), (0, 0, 1), (0, 7, 1), (0, 3, 1), (0, 5, 1))
+BACK = ((1, 2), (4, 1), (6, 1))
 
 
 def kernel(
     cells, per_group,
-    x, vec, w, out,
+    x, gain, bias, cbias, w, out,
     xo, xr, act_a, act_b, act_c, act_d, wv, z, ind, tm_out, tm_in, row_out, row_in, hop1, hop2, gv,
     load_sem, wsem, vec_sem,
     bulk_send, bulk_recv, back_send, back_recv, halo_send, halo_recv, fwd_send, fwd_recv,
@@ -32,8 +32,12 @@
 
     load = pltpu.make_async_copy(x.at[0], xo.at[:, 1 : height + 1], load_sem)
     load.start()
-    vector = pltpu.make_async_copy(vec, gv, vec_sem)
-    vector.start()
+    vectors = [
+        pltpu.make_async_copy(v, gv.at[pl.ds(i * ch, ch)], vec_sem.at[i])
+        for i, v in enumerate((gain, bias, cbias))
+    ]
+    for c in vectors:
+        c.start()
     wloads = [
         pltpu.make_async_copy(w.at[:, :, kw], wv.at[:, :, :, pl.ds(kw * ch, ch)], wsem.at[kw])
         for kw in range(3)
@@ -175,7 +179,8 @@
     off = channel_mean - mean
     square = over_group(square + (pixels * n_tm * n_rows) * (off * off))
     inverse = lax.rsqrt(square * (1.0 / cells) + EPS)
-    vector.wait()
+    for c in vectors:
+        c.wait()
     scale = 0.5 * (inverse * gv[pl.ds(0, ch)].reshape(1, ch))
     shift = 0.5 * gv[pl.ds(ch, ch)].reshape(1, ch)
 
@@ -300,6 +305,7 @@
         norms(xo, 0, act_c, high) + norms(xo, 1, act_d, high),
     )
     pass_back(1, 1)
+    pass_back(1, 2)
     edges_in(1)
     run(
         pair(act_c, (2, 1), half, half, False)
@@ -319,6 +325,7 @@
             + pair(act_b, (1, 0), 0, half, True)
         )
         pass_back(2, 1)
+        pass_back(2, 2)
         bulk(3).wait_recv()
         run(norms(xr, 1, act_b, (6, 7)))
         run(
@@ -333,19 +340,21 @@
             norms(xr, 0, act_a, (8,)) + finishes(1, half, half),
         )
         bulk(6).wait_recv()
+        back(2, 1).wait_recv()
         run(norms(xr, 0, act_a, (4,)))
         run(
-            some(3, 1, (1,)) + some(2, 1, (2,)) + some(4, 1, (0,)) + some(6, 1, (2,)) + some(7, 1, (1,)),
-            finishes(0, 1, 2),
+            some(2, 1, (2,)) + some(6, 1, (2,)) + some(3, 1, (1, 2)) + some(4, 1, (0, 1))
+            + some(5, 1, (0,)) + some(7, 1, (1,)),
+            norms(xr, 0, act_a, (5,)) + finishes(0, 1, 2),
         )
         bulk(7).wait_recv()
-        back(2, 1).wait_recv()
+        back(2, 2).wait_recv()
         edges_in(0)
-        run(norms(xr, 0, act_a, (5, 0)))
-        run(some(3, 1, (2,)) + some(0, 1, (0,)), norms(xr, 0, act_a, (6, 7, 9)))
-        run(some(4, 1, (1, 2)), finishes(0, 0, 1))
-        run(some(5, 1, (0, 1, 2)), finishes(0, 3, 2))
-        run(some(6, 1, (0, 1)), finishes(0, 5, 1))
+        run(norms(xr, 0, act_a, (6,)))
+        run(some(4, 1, (2,)), norms(xr, 0, act_a, (7, 0, 9)) + finishes(0, 3, 1))
+        run(some(5, 1, (1, 2)), finishes(0, 4, 1))
+        run(some(0, 1, (0,)), finishes(0, 5, 1))
+        run(some(6, 1, (0, 1)), finishes(0, 0, 1))
         run(some(7, 1, (0, 2)), finishes(0, 6, 1))
         run(finishes(0, 7, 1))
 
@@ -353,11 +362,10 @@
     def _():
         run(main(0, (act_c,), 2, half, half, False))
         pass_back(2, 1)
+        pass_back(2, 2)
         for t in range(frames):
             run(finishes(t, 0, height))
-        forward(0)
-        edges_in(0)
-        for i in (2, 3, 6, 7):
+        for i in range(2, len(PIECES)):
             bulk(i).wait_recv()
         for p in range(len(BACK)):
             back(2, p).wait_recv()
@@ -369,8 +377,11 @@
             back(hop, p).wait_send()
     for i in range(2):
         own_edge(i).wait_send()
-        for f in range(2):
-            fwd_edge(f, i).wait_send()
+        fwd_edge(1, i).wait_send()
+
+        @pl.when(recvs_on)
+        def _():
+            fwd_edge(0, i).wait_send()
 
 
 def shards(inputs, norm_gain, norm_bias, conv_weight, conv_bias):
@@ -385,7 +396,7 @@
     return pl.pallas_call(
         functools.partial(kernel, cells, per_group),
         out_shape=jax.ShapeDtypeStruct(inputs.shape, BF16),
-        in_specs=[hbm] * 3,
+        in_specs=[hbm] * 5,
         out_specs=pl.BlockSpec(memory_space=pltpu.VMEM),
         scratch_shapes=[
             pltpu.VMEM((frames, height + 2, width, ch), BF16),
@@ -406,7 +417,7 @@
             pltpu.VMEM((3 * ch,), F32),
             pltpu.SemaphoreType.DMA,
             dma(3),
-            pltpu.SemaphoreType.DMA,
+            dma(3),
             dma(len(PIECES)),
             dma(len(PIECES)),
             dma(3 * len(BACK)),
@@ -423,7 +434,9 @@
         compiler_params=pltpu.CompilerParams(
             collective_id=0, has_side_effects=True, vmem_limit_bytes=51 * 1024 * 1024
         ),
-    )(inputs, jnp.concatenate([norm_gain, norm_bias, conv_bias]), conv_weight)
+    )(
+        inputs, *(pltpu.with_memory_space_constraint(v, pltpu.HBM) for v in (norm_gain, norm_bias, conv_bias)), conv_weight
+    )
 
 
 def solution(mesh):

time: 35.9 us -> 35.1 us (0.978)
  other arithmetic: 0.72 us -> 0 us
    concatenate x1 -> x0, other arithmetic: 0.72 us -> none  [shards(): jnp.concatenate([norm_gain, norm_bias, conv_bias])]
where the time goes in v6:
time: 35.1 us; the launch traced here: 35 us
  Pallas kernels  33.8 us (96%)
  local copies, waits for them, and re-layouts  1.15 us (3%)
    pallas_call x1, Pallas kernels, shards(): pl.pallas_call(functools.partial(kernel, cells, per_group), out_shape=jax...  33.8 us
    unnamed x1, local copies, waits for them, and re-layouts  1.15 us

profile of v6, /device:TPU:99, one launch (start us, length us, event | category | flops | bytes accessed | tf_op | source)
XLA Modules:
  0.0 35.0 jit_solution(14925046236775327175)
XLA Ops:
  0.0 33.8 %shard_map.55 = bf16[1,2,8,128,384]{4,3,2,1,0:T(8,128)(2,1)S(1)} custom-call(bf16[1,2,8,128,384]{4,3,2,1,0:T(8,128)(2,1)} %x.1, f32[384]{0:T(512)} %gain.1, f32[384]{0:T(512)} %bias.1, f32[384]{0:T(512)} %cbias.1, bf16[3,3,3,384,384]{4,3,2,1,0:T(8,128)(2,1)} %w.1), custom_call_target="tpu_custom_call" | custom-call | tf_op jit(solution)/shard_map/pallas_call | solution.py:396
  33.8 1.1 %copy.7 = bf16[1,2,8,128,384]{4,3,2,1,0:T(8,128)(2,1)} copy(bf16[1,2,8,128,384]{4,3,2,1,0:T(8,128)(2,1)S(1)} %shard_map.55) | data formatting | bytes 3145728

commit v7 on v6

--- a/solution.py
+++ b/solution.py
@@ -288,6 +288,16 @@
         fwd_edge(f, 0).wait_recv()
         fwd_edge(f, 1).wait_recv()
 
+    def early_sends():
+        for i in range(len(PIECES) - 1):
+            bulk(i).wait_send()
+        for hop in range(2):
+            for p in range(len(BACK)):
+                back(hop, p).wait_send()
+        for i in range(2):
+            own_edge(i).wait_send()
+            fwd_edge(1, i).wait_send()
+
     low, high = range(0, half + 2), range(half + 2, height + 2)
     forward(1)
     own_edge(0).wait_recv()
@@ -347,6 +357,7 @@
             + some(5, 1, (0,)) + some(7, 1, (1,)),
             norms(xr, 0, act_a, (5,)) + finishes(0, 1, 2),
         )
+        early_sends()
         bulk(7).wait_recv()
         back(2, 2).wait_recv()
         edges_in(0)
@@ -365,22 +376,19 @@
         pass_back(2, 2)
         for t in range(frames):
             run(finishes(t, 0, height))
+        early_sends()
         for i in range(2, len(PIECES)):
             bulk(i).wait_recv()
         for p in range(len(BACK)):
             back(2, p).wait_recv()
 
-    for i in range(len(PIECES)):
-        bulk(i).wait_send()
-    for hop in range(3):
-        for p in range(len(BACK)):
-            back(hop, p).wait_send()
-    for i in range(2):
-        own_edge(i).wait_send()
-        fwd_edge(1, i).wait_send()
-
-        @pl.when(recvs_on)
-        def _():
+    bulk(len(PIECES) - 1).wait_send()
+    for p in range(len(BACK)):
+        back(2, p).wait_send()
+
+    @pl.when(recvs_on)
+    def _():
+        for i in range(2):
             fwd_edge(0, i).wait_send()
 
 

time: 35.1 us -> 35.1 us (level)
  no operation moved by 1% of the time
where the time goes in v7:
time: 35.1 us; the launch traced here: 35 us
  Pallas kernels  33.8 us (96%)
  local copies, waits for them, and re-layouts  1.15 us (3%)
    pallas_call x1, Pallas kernels, shards(): pl.pallas_call(functools.partial(kernel, cells, per_group), out_shape=jax...  33.8 us
    unnamed x1, local copies, waits for them, and re-layouts  1.15 us

profile of v7, /device:TPU:99, one launch (start us, length us, event | category | flops | bytes accessed | tf_op | source)
XLA Modules:
  0.0 35.0 jit_solution(14041874407155649055)
XLA Ops:
  0.0 33.8 %shard_map.55 = bf16[1,2,8,128,384]{4,3,2,1,0:T(8,128)(2,1)S(1)} custom-call(bf16[1,2,8,128,384]{4,3,2,1,0:T(8,128)(2,1)} %x.1, f32[384]{0:T(512)} %gain.1, f32[384]{0:T(512)} %bias.1, f32[384]{0:T(512)} %cbias.1, bf16[3,3,3,384,384]{4,3,2,1,0:T(8,128)(2,1)} %w.1), custom_call_target="tpu_custom_call" | custom-call | tf_op jit(solution)/shard_map/pallas_call | solution.py:404
  33.8 1.1 %copy.7 = bf16[1,2,8,128,384]{4,3,2,1,0:T(8,128)(2,1)} copy(bf16[1,2,8,128,384]{4,3,2,1,0:T(8,128)(2,1)S(1)} %shard_map.55) | data formatting | bytes 3145728
